TPU v7x, 32 devices: a whole 2x2x4 slice. The times are simulated.
32 devices in a mesh: sess: 16 (over z, x, core), exp: 2 (over y).
Axes of the slice: x: 2, y: 2, z: 4, core: 2. Of those that a mesh axis runs over, the one named last changes fastest.
Arguments:
- tokens: bfloat16 [16, 64, 4096], P('sess'), may hold values from -6 to 6
- routes: int32 [16, 64, 2], P('sess'), may hold values from 0 to 15, all different within a row; in each aligned block of 64 rows (0 to 63, 64 to 127, ..., all dimensions but the last counted through in order) at most 16 rows name the same one
- gates: float32 [16, 64, 2], P('sess'), may hold values from 0.2 to 1
- w_gate: bfloat16 [16, 4096, 1408], P('sess', None, 'exp'), may hold values from -0.09375 to 0.09375
- w_up: bfloat16 [16, 4096, 1408], P('sess', None, 'exp'), may hold values from -0.09375 to 0.09375
- w_down: bfloat16 [16, 1408, 4096], P('sess', 'exp'), may hold values from -0.15625 to 0.15625
- feat_gain: float32 [4096], replicated, may hold values from 0.25 to 1.75
- w_proj: bfloat16 [4096, 256], replicated, may hold values from -0.09375 to 0.09375
- conv_time: bfloat16 [3, 3, 3, 256, 256], replicated, may hold values from -0.078125 to 0.078125
- bias_time: float32 [256], replicated, may hold values from -3 to 3
- conv_space: bfloat16 [3, 3, 256, 256], replicated, may hold values from -0.125 to 0.125
- bias_space: float32 [256], replicated, may hold values from -3 to 3
- frame_cache: bfloat16 [3, 16, 16, 16, 256], P(None, 'sess', 'exp'), may hold values from -6 to 6
- cache_head: int32 [16], P('sess'), may hold values from 0 to 2
Outputs:
- out_frame: bfloat16 [16, 16, 16, 256], P('sess', 'exp')
Inputs may be any that keep to these rules, and one draw needn't show every extreme that they name: `routes`: each token names 2 different experts; among the tokens of one session no expert is named more than 16 times, and in some sessions one is named exactly 16 times. The frame before the previous one is in slot (cache_head + 2) mod 3.
All inputs are finite; a program needn't handle non-finite values.
Results may differ from a plain program's by a relative error of at most 0.017.
Values may be sent and summed in bfloat16 or wider, within the bound.
A program may use at most 64 MiB of HBM per device.

v0:
```python
import jax
import jax.numpy as jnp
from jax import lax
from jax.sharding import PartitionSpec as P

TOPK = 2
GRID_W = 8
TROW = 4


epsilon = 1e-06


def extended(cells, sides, width):
    for axis, dim in sides:
        count = lax.axis_size(axis)
        ends = count - 1
        head = lax.slice_in_dim(cells, 0, width, axis=dim)
        tail = lax.slice_in_dim(cells, cells.shape[dim] - width, cells.shape[dim], axis=dim)
        cells = jnp.concatenate(
            [
                lax.ppermute(tail, axis, [(i, (i + 1) % count) for i in range(ends)]),
                cells,
                lax.ppermute(head, axis, [((i + 1) % count, i) for i in range(ends)]),
            ],
            axis=dim,
        )
    return cells


def slot_targets(routes, experts, capacity):
    flat = routes.reshape(-1)
    onehot = (flat[:, None] == jnp.arange(experts, dtype=jnp.int32)[None, :]).astype(jnp.int32)
    before = jnp.cumsum(onehot, axis=0) - onehot
    position = jnp.sum(before * onehot, axis=1)
    return flat * capacity + position


def pick_slot(cache, heads):
    choose = (jnp.arange(3, dtype=jnp.int32)[:, None] == heads[None, :]).astype(jnp.float32)
    return jnp.sum(choose[:, :, None, None, None] * cache.astype(jnp.float32), axis=0).astype(
        jnp.bfloat16
    )


def expert_rows(rows, w_gate, w_up, w_down):
    leading = rows.shape[:-1]
    flat_rows = rows.reshape(-1, rows.shape[-1])
    gate = jnp.dot(flat_rows, w_gate[0], preferred_element_type=jnp.float32)
    upward = jnp.dot(flat_rows, w_up[0], preferred_element_type=jnp.float32)
    hidden = (jax.nn.silu(gate) * upward).astype(jnp.bfloat16)
    output = jnp.dot(hidden, w_down[0], preferred_element_type=jnp.float32).astype(jnp.bfloat16)
    return output.reshape(leading + (output.shape[-1],))


def space_patches(field, height, breadth):
    return jnp.concatenate(
        [
            field[:, row_step : row_step + height, col_step : col_step + breadth, :]
            for row_step in range(3)
            for col_step in range(3)
        ],
        axis=-1,
    )


def time_patches(frames, height, breadth):
    return jnp.concatenate(
        [space_patches(frames[frame_step], height, breadth) for frame_step in range(3)], axis=-1
    )


def apply_kernel(patches, kernel):
    channels = kernel.shape[-1]
    return jnp.dot(
        patches.reshape(-1, patches.shape[-1]),
        kernel.reshape(-1, channels),
        preferred_element_type=jnp.float32,
    )


def body(
    tokens,
    routes,
    gates,
    w_gate,
    w_up,
    w_down,
    feat_gain,
    w_proj,
    conv_time,
    bias_time,
    conv_space,
    bias_space,
    frame_cache,
    cache_head,
):
    sess_count = lax.axis_size("sess")
    tile = lax.axis_index("exp")
    width = tokens.shape[-1]
    channels = w_proj.shape[-1]
    local = tokens[0]
    tok_count = local.shape[0]
    capacity = 2 * tok_count * TOPK // sess_count
    rows_own = TROW * GRID_W
    count = tok_count * TOPK
    dest = slot_targets(routes[0], sess_count, capacity)
    source = jnp.arange(count, dtype=jnp.int32) // TOPK
    weight_rows = gates[0].reshape(count, 1)
    outgoing = jnp.zeros((sess_count * capacity, width), jnp.bfloat16).at[dest].set(local[source])
    outgoing = outgoing.reshape(sess_count, capacity, width)
    answer = expert_rows(
        lax.all_to_all(outgoing, "sess", split_axis=0, concat_axis=0, tiled=True),
        w_gate,
        w_up,
        w_down,
    )
    returned = lax.all_to_all(answer, "sess", split_axis=0, concat_axis=0, tiled=True).reshape(
        sess_count * capacity, width
    )
    combined = jnp.sum(
        (returned[dest].astype(jnp.float32) * weight_rows).reshape(-1, TOPK, width), axis=1
    )
    summed = lax.psum_scatter(
        combined.astype(jnp.bfloat16), "exp", scatter_dimension=0, tiled=True
    ).astype(jnp.float32)
    own = lax.dynamic_slice_in_dim(local, tile * rows_own, rows_own, 0)
    feat = (own.astype(jnp.float32) + summed).astype(jnp.bfloat16)
    square = jnp.mean(jnp.square(feat.astype(jnp.float32)), axis=-1, keepdims=True)
    normed = (feat.astype(jnp.float32) * lax.rsqrt(square + epsilon) * feat_gain).astype(
        jnp.bfloat16
    )
    coarse = jnp.dot(normed, w_proj, preferred_element_type=jnp.float32).astype(jnp.bfloat16)
    coarse = coarse.reshape(1, TROW, GRID_W, channels)
    fine = jnp.repeat(jnp.repeat(coarse, 2, axis=1), 2, axis=2)
    latest = pick_slot(frame_cache, cache_head)
    older = pick_slot(frame_cache, (cache_head + 2) % 3)
    stack = jnp.stack([older, latest, fine])
    height = fine.shape[1]
    breadth = fine.shape[2]
    framed = extended(stack, (("exp", 2),), 1)
    framed = jnp.pad(framed, ((0, 0), (0, 0), (0, 0), (1, 1), (0, 0)))
    first = apply_kernel(time_patches(framed, height, breadth), conv_time) + bias_time
    active = jax.nn.silu(first).astype(jnp.bfloat16).reshape(-1, height, breadth, channels)
    bordered = extended(active, (("exp", 1),), 1)
    bordered = jnp.pad(bordered, ((0, 0), (0, 0), (1, 1), (0, 0)))
    second = apply_kernel(space_patches(bordered, height, breadth), conv_space)
    result = fine.astype(jnp.float32).reshape(-1, channels) + second + bias_space
    return result.astype(jnp.bfloat16).reshape(fine.shape)


def solution(mesh):
    return jax.shard_map(
        body,
        mesh=mesh,
        in_specs=(
            P("sess", None, None),
            P("sess", None, None),
            P("sess", None, None),
            P("sess", None, "exp"),
            P("sess", None, "exp"),
            P("sess", "exp", None),
            P(),
            P(),
            P(),
            P(),
            P(),
            P(),
            P(None, "sess", "exp", None, None),
            P("sess"),
        ),
        out_specs=P("sess", "exp", None, None),
        check_vma=False,
    )
```

profile of v0, /device:TPU:0, one launch (start us, length us, event | category | flops | bytes accessed | tf_op | source)
XLA Modules:
  0.0 214.0 jit_solution(18081297043925421091)
XLA Ops:
  6.5 0.0 copy-start
  6.5 1.5 copy.19
  8.1 0.7 broadcast_multiply_fusion
  8.8 0.9 eq.49
  9.7 0.7 fusion.46
  10.4 1.6 reduce_window_sum.11
  12.0 1.0 select_reduce_fusion
  13.0 0.7 copy.18
  13.7 0.9 mul.79
  14.6 7.0 %scatter_custom_fusion = bf16[256,4096]{1,0:T(8,128)(2,1)} fusion(s32[128]{0:T(128)S(1)} %fusion.48, bf16[64,4096]{1,0:T(8,128)(2,1)} %bitcast.92, s32[1024]{0:T(1024)S(1)} %pad_clamp_fusion.1, bf16[]{:T(256)} %constant.55.clone.1), kind=kCustom, calls=%fused_computation.21 | custom fusion | bytes 2097664 | tf_op jit(solution)/shard_map/scatter | solution.py:110
  21.6 54.5 %all_to_all.10 = bf16[16,16,4096]{2,1,0:T(8,128)(2,1)S(1)} all-to-all(bf16[16,16,4096]{2,1,0:T(8,128)(2,1)} %bitcast.79), channel_id=1, replica_groups=mesh['sess'=16,'exp'=2] {'sess'}, dimensions={0} | all-to-all | bytes 4194304 | tf_op jit(solution)/shard_map/all_to_all | solution.py:113
  76.1 0.0 copy-start.1
  76.1 1.3 copy-done.1
  77.4 5.2 %fusion.4 = f32[256,704]{0,1:T(8,128)} fusion(bf16[256,4096]{1,0:T(8,128)(2,1)S(1)} %bitcast.81, bf16[1,4096,704]{1,2,0:T(8,128)(2,1)} %param.17), kind=kOutput, calls=%fused_computation.7 | convolution fusion | flops 1476395008 | bytes 8585216 | tf_op jit(solution)/shard_map/dot_general | solution.py:49
  82.6 12.8 %fusion.6 = bf16[256,4096]{1,0:T(8,128)(2,1)} fusion(bf16[1,704,4096]{2,1,0:T(8,128)(2,1)} %param.19, bf16[256,4096]{1,0:T(8,128)(2,1)} %bitcast.82, bf16[1,4096,704]{1,2,0:T(8,128)(2,1)} %param.18, f32[256,704]{0,1:T(8,128)} %fusion.4), kind=kOutput, calls=%fused_computation.9 | convolution fusion | flops 2954919936 | bytes 16449536 | tf_op jit(solution)/shard_map/dot_general | solution.py:52
  95.5 0.0 copy-start.7
  95.5 5.3 %all-to-all-start.1 = ((bf16[16,16,4096]{2,1,0:T(8,128)(2,1)}), bf16[16,16,4096]{2,1,0:T(8,128)(2,1)}, u32[]{:S(2)}, u32[]{:S(2)}) async-start(bf16[16,16,4096]{2,1,0:T(8,128)(2,1)} %bitcast.80), calls=%async_computation.1 | async-start | bytes 4194304 | tf_op jit(solution)/shard_map/all_to_all | solution.py:118
  100.8 0.0 reduce-scatter.2.cloned.1.call-start
  100.9 0.0 copy-done.7
  100.9 0.7 copy.20
  101.6 40.3 %all-to-all-done.1 = bf16[16,16,4096]{2,1,0:T(8,128)(2,1)} async-done(((bf16[16,16,4096]{2,1,0:T(8,128)(2,1)}), bf16[16,16,4096]{2,1,0:T(8,128)(2,1)}, u32[]{:S(2)}, u32[]{:S(2)}) %all-to-all-start.1) | async-done | bytes 2097184 | tf_op jit(solution)/shard_map/all_to_all | solution.py:118
  141.8 5.0 %gather_fusion = bf16[128,4096]{1,0:T(8,128)(2,1)} fusion(bf16[256,4096]{1,0:T(8,128)(2,1)} %bitcast.11, s32[1024]{0:T(1024)S(1)} %pad_clamp_fusion), kind=kCustom, calls=%fused_computation.1 | custom fusion | bytes 2097664 | tf_op jit(solution)/shard_map/gather | solution.py:122
  146.9 3.4 %reshape.215 = f32[64,2,4096]{2,1,0:T(2,128)} reshape(bf16[128,4096]{1,0:T(8,128)(2,1)} %gather_fusion) | data formatting | bytes 3145728 | tf_op jit(solution)/shard_map/convert_element_type | solution.py:122
  150.3 5.6 %multiply_reduce_fusion = bf16[64,4096]{1,0:T(8,128)(2,1)} fusion(f32[64,2,4096]{2,1,0:T(2,128)} %reshape.215, f32[64,2]{1,0:T(8,128)} %copy.20), kind=kLoop, calls=%fused_computation.10 | loop fusion | flops 786432 | bytes 2621952 | tf_op jit(solution)/shard_map/reduce_sum | solution.py:121
  155.8 0.0 reduce-scatter.2.cloned.1.call-update
  156.5 1.8 fusion.28
  158.3 18.9 %reduce-scatter.2.cloned.1.call-done = bf16[32,4096]{1,0:T(8,128)(2,1)} async-done(((bf16[64,4096]{1,0:T(8,128)(2,1)}), bf16[32,4096]{1,0:T(8,128)(2,1)}) %reduce-scatter.2.cloned.1.call-update) | async-done | bytes 262160 | tf_op jit(solution)/shard_map/reduce_scatter | solution.py:124
  177.2 1.2 fusion.24
  178.4 2.3 %fusion.17 = bf16[4,8,256]{2,1,0:T(8,128)(2,1)S(1)} fusion(bf16[4096,256]{1,0:T(8,128)(2,1)} %param.21, f32[4096]{0:T(1024)} %param.20, f32[32]{0:T(128)S(1)} %add_rsqrt_fusion, bf16[32,4096]{1,0:T(8,128)(2,1)} %reduce-scatter.2.cloned.1.call-done, bf16[1,64,4096]{2,1,0:T(8,128)(2,1)} %param.14, s32[]{:T(128)S(6)} %select_n.43), kind=kOutput, calls=%fused_computation.18 | convolution fusion | flops 68165632 | bytes 2654340 | tf_op jit(solution)/shard_map/dot_general | solution.py:133
  180.8 0.7 broadcast_in_dim.16
  181.4 1.5 broadcast_in_dim.34
  182.9 0.8 pad_maximum_fusion.4
  183.7 2.2 %collective-permute-start = (bf16[3,1,1,16,256]{4,3,2,1,0:T(8,128)(2,1)S(1)}, bf16[3,1,1,16,256]{4,3,2,1,0:T(8,128)(2,1)S(1)}, u32[]{:S(2)}, u32[]{:S(2)}) collective-permute-start(bf16[3,1,1,16,256]{4,3,2,1,0:T(8,128)(2,1)S(1)} %get-tuple-element.10), channel_id=1, source_target_pairs={{0,1},{2,3},{4,5},{6,7},{8,9},{10,11},{12,13},{14,15},{16,17},{18,... | collective-permute-start | bytes 73736 | tf_op jit(solution)/shard_map/ppermute | solution.py:22
  185.9 1.3 collective-permute-start.1
  187.2 0.2 collective-permute-done
  187.4 4.2 %collective-permute-done.1 = bf16[3,1,1,16,256]{4,3,2,1,0:T(8,128)(2,1)S(1)} collective-permute-done((bf16[3,1,1,16,256]{4,3,2,1,0:T(8,128)(2,1)S(1)}, bf16[3,1,1,16,256]{4,3,2,1,0:T(8,128)(2,1)S(1)}, u32[]{:S(2)}, u32[]{:S(2)}) %collective-permute-start.1) | collective-permute-done | bytes 24608 | tf_op jit(solution)/shard_map/ppermute | solution.py:24
  191.7 1.1 select_maximum_fusion
  192.8 0.0 copy-start.6
  193.5 0.0 copy-done
  193.5 0.0 copy-done.6
  193.5 0.7 multiply_convert_fusion
  194.2 0.0 copy-start.2
  194.2 0.6 copy-done.2
  194.8 0.6 fusion.52
  195.4 2.2 %collective-permute-start.2 = (bf16[1,1,16,256]{3,2,1,0:T(8,128)(2,1)}, bf16[1,1,16,256]{3,2,1,0:T(8,128)(2,1)}, u32[]{:S(2)}, u32[]{:S(2)}) collective-permute-start(bf16[1,1,16,256]{3,2,1,0:T(8,128)(2,1)} %get-tuple-element.20), channel_id=1, source_target_pairs={{0,1},{2,3},{4,5},{6,7},{8,9},{10,11},{12,13},{14,15},{16,17},{18,... | collective-permute-start | bytes 24584 | tf_op jit(solution)/shard_map/ppermute | solution.py:22
  197.6 1.3 collective-permute-start.3
  198.9 0.7 broadcast_in_dim.15
  199.6 1.6 convert_element_type.127
  201.2 0.0 copy-start.3
  201.2 0.0 copy-start.4
  201.2 0.0 copy-start.5
  201.2 0.0 collective-permute-done.2
  201.2 2.2 %collective-permute-done.3 = bf16[1,1,16,256]{3,2,1,0:T(8,128)(2,1)} collective-permute-done((bf16[1,1,16,256]{3,2,1,0:T(8,128)(2,1)}, bf16[1,1,16,256]{3,2,1,0:T(8,128)(2,1)}, u32[]{:S(2)}, u32[]{:S(2)}) %collective-permute-start.3) | collective-permute-done | bytes 8224 | tf_op jit(solution)/shard_map/ppermute | solution.py:24
  203.5 0.9 fusion.44
  204.4 0.9 pad_maximum_fusion
  205.4 0.0 copy-done.3
  205.5 0.0 copy-done.4
  205.5 0.0 copy-done.5
  205.5 1.6 fusion.16
  (46 shorter events, 0.6 us)
Async XLA Ops:
  6.5 186.9 %copy-start = (bf16[3,3,3,256,256]{4,3,2,1,0:T(8,128)(2,1)S(1)}, bf16[3,3,3,256,256]{4,3,2,1,0:T(8,128)(2,1)}, u32[]{:S(2)}) copy-start(bf16[3,3,3,256,256]{4,3,2,1,0:T(8,128)(2,1)} %param.22) | copy-start | bytes 10616836
  76.1 1.3 copy-start.1
  95.5 5.4 %copy-start.7 = (f32[1,64,2]{1,2,0:T(2,128)S(1)}, f32[1,64,2]{1,2,0:T(2,128)}, u32[]{:S(2)}) copy-start(f32[1,64,2]{1,2,0:T(2,128)} %param.16) | copy-start | bytes 1540
  95.5 46.4 %all-to-all-start.1 = ((bf16[16,16,4096]{2,1,0:T(8,128)(2,1)}), bf16[16,16,4096]{2,1,0:T(8,128)(2,1)}, u32[]{:S(2)}, u32[]{:S(2)}) async-start(bf16[16,16,4096]{2,1,0:T(8,128)(2,1)} %bitcast.80), calls=%async_computation.1 | async-start | bytes 4194304 | tf_op jit(solution)/shard_map/all_to_all | solution.py:118
  100.8 76.4 %reduce-scatter.2.cloned.1.call-start = ((), (), s32[]{:S(2)}) async-start(), calls=%async_computation.3 | async-start | bytes 786432 | tf_op jit(solution)/shard_map/reduce_scatter | solution.py:124
  183.7 3.8 %collective-permute-start = (bf16[3,1,1,16,256]{4,3,2,1,0:T(8,128)(2,1)S(1)}, bf16[3,1,1,16,256]{4,3,2,1,0:T(8,128)(2,1)S(1)}, u32[]{:S(2)}, u32[]{:S(2)}) collective-permute-start(bf16[3,1,1,16,256]{4,3,2,1,0:T(8,128)(2,1)S(1)} %get-tuple-element.10), channel_id=1, source_target_pairs={{0,1},{2,3},{4,5},{6,7},{8,9},{10,11},{12,13},{14,15},{16,17},{18,... | collective-permute-start | bytes 73736 | tf_op jit(solution)/shard_map/ppermute | solution.py:22
  185.9 5.7 %collective-permute-start.1 = (bf16[3,1,1,16,256]{4,3,2,1,0:T(8,128)(2,1)S(1)}, bf16[3,1,1,16,256]{4,3,2,1,0:T(8,128)(2,1)S(1)}, u32[]{:S(2)}, u32[]{:S(2)}) collective-permute-start(bf16[3,1,1,16,256]{4,3,2,1,0:T(8,128)(2,1)S(1)} %get-tuple-element.11), channel_id=1, source_target_pairs={{1,0},{3,2},{5,4},{7,6},{9,8},{11,10},{13,12},{15,14},{17,16},{19,... | collective-permute-start | bytes 73736 | tf_op jit(solution)/shard_map/ppermute | solution.py:24
  192.8 0.7 copy-start.6
  194.2 0.6 copy-start.2
  195.4 5.8 %collective-permute-start.2 = (bf16[1,1,16,256]{3,2,1,0:T(8,128)(2,1)}, bf16[1,1,16,256]{3,2,1,0:T(8,128)(2,1)}, u32[]{:S(2)}, u32[]{:S(2)}) collective-permute-start(bf16[1,1,16,256]{3,2,1,0:T(8,128)(2,1)} %get-tuple-element.20), channel_id=1, source_target_pairs={{0,1},{2,3},{4,5},{6,7},{8,9},{10,11},{12,13},{14,15},{16,17},{18,... | collective-permute-start | bytes 24584 | tf_op jit(solution)/shard_map/ppermute | solution.py:22
  197.6 5.8 %collective-permute-start.3 = (bf16[1,1,16,256]{3,2,1,0:T(8,128)(2,1)}, bf16[1,1,16,256]{3,2,1,0:T(8,128)(2,1)}, u32[]{:S(2)}, u32[]{:S(2)}) collective-permute-start(bf16[1,1,16,256]{3,2,1,0:T(8,128)(2,1)} %get-tuple-element.21), channel_id=1, source_target_pairs={{1,0},{3,2},{5,4},{7,6},{9,8},{11,10},{13,12},{15,14},{17,16},{19,... | collective-permute-start | bytes 24584 | tf_op jit(solution)/shard_map/ppermute | solution.py:24
  201.2 4.1 %copy-start.3 = (bf16[128,256]{1,0:T(8,128)(2,1)S(1)}, bf16[128,256]{1,0:T(8,128)(2,1)}, u32[]{:S(2)}) copy-start(bf16[128,256]{1,0:T(8,128)(2,1)} %copy-done.2) | copy-start | bytes 196612
  201.2 4.2 %copy-start.4 = (bf16[3,3,256,256]{3,2,1,0:T(8,128)(2,1)S(1)}, bf16[3,3,256,256]{3,2,1,0:T(8,128)(2,1)}, u32[]{:S(2)}) copy-start(bf16[3,3,256,256]{3,2,1,0:T(8,128)(2,1)} %param.24) | copy-start | bytes 3538948
  201.2 4.2 %copy-start.5 = (f32[128,256]{1,0:T(8,128)S(1)}, f32[128,256]{1,0:T(8,128)}, u32[]{:S(2)}) copy-start(f32[128,256]{1,0:T(8,128)} %convert_element_type.127) | copy-start | bytes 393220
Sparse Core Ops, SparseCore 0:
  156.0 21.2 reduce-scatter.1
where the time goes:
time: 215 us; the launch traced here: 214 us
  waiting for transfers between devices  65.8 us (31%)
  blocking collectives  54.5 us (25%)
  local copies, waits for them, and re-layouts  27.7 us (13%)
  matrix products  22.6 us (11%)
  other arithmetic  16.3 us (8%)
  between operations  14.5 us (7%)
  starting transfers between devices  12.4 us (6%)
    all_to_all x1, blocking collectives, body(): lax.all_to_all(outgoing, 'sess', split_axis=0, concat_axis=0, tiled=True)  54.5 us
    all_to_all x1, waiting for transfers between devices, body(): lax.all_to_all(answer, 'sess', split_axis=0, concat_axis=0, tiled=True)  40.3 us
    reduce_scatter x1, waiting for transfers between devices, body(): lax.psum_scatter(combined.astype(jnp.bfloat16), 'exp', scatter_dimension=...  18.9 us
    dot_general x1, matrix products, expert_rows(): jnp.dot(hidden, w_down[0], preferred_element_type=jnp.float32)  12.8 us
    scatter x1, local copies, waits for them, and re-layouts, body(): jnp.zeros((sess_count * capacity, width), jnp.bfloat16).at[dest]  6.98 us
    ppermute x2, waiting for transfers between devices, extended(): lax.ppermute(head, axis, [((i + 1) % count, i) for i in range(ends)])  6.43 us
    reduce_sum x1, other arithmetic, body(): jnp.sum((returned[dest].astype(jnp.float32) * weight_rows).reshape(-1, TO...  5.55 us
    all_to_all x1, starting transfers between devices, body(): lax.all_to_all(answer, 'sess', split_axis=0, concat_axis=0, tiled=True)  5.33 us
  transfers between devices with their start and end apart: 6, of which 5 were waited for; matrix products, arithmetic and copies ran while one was open for 2% of the time, Pallas kernels for 0%

commit v1 on v0

v1 whole, which is shorter than its diff:
```python
import functools

import jax
import jax.numpy as jnp
from jax import lax
from jax.experimental import pallas as pl
from jax.experimental.pallas import tpu as pltpu
from jax.sharding import PartitionSpec as P

TOPK = 2
GRID_W = 8
HALO = 2
MESH = pl.DeviceIdType.MESH
VMEM = pl.BlockSpec(memory_space=pltpu.VMEM)

epsilon = 1e-06


def partner(me, bits):
    other, weight = me, 1
    while bits:
        if bits & 1:
            other = other + weight * (1 - 2 * ((me // weight) % 2))
        bits //= 2
        weight *= 2
    return other


def exchange_order(count):
    near = min(4, count)
    order = [k for k in range(1, near)]
    for low in range(near):
        for high in range(count // near - 1, 0, -1):
            order.append(high * near + low)
    return order


def enter(me, tile, sessions, tiles):
    barrier = pltpu.get_barrier_semaphore()
    for k in range(1, sessions):
        pl.semaphore_signal(barrier, inc=1, device_id=(partner(me, k), tile), device_id_type=MESH)
    for m in range(1, tiles):
        pl.semaphore_signal(
            barrier, inc=1, device_id=(me, (tile + m) % tiles), device_id_type=MESH
        )
    pl.semaphore_wait(barrier, sessions - 1 + tiles - 1)


def dispatch_kernel(sessions, tiles, cap, src, out, own_sem, send1, recv1, send2, recv2):
    me, tile = lax.axis_index("sess"), lax.axis_index("exp")
    width = src.shape[1]
    part = width // tiles
    columns = pl.ds(pl.multiple_of(tile * part, part), part)

    def rows(index):
        return pl.ds(pl.multiple_of(index * cap, cap), cap)

    enter(me, tile, sessions, tiles)
    own = pltpu.make_async_copy(src.at[rows(me), :], out.at[rows(me), :], own_sem)
    own.start()
    order = exchange_order(sessions)
    copies = {}
    for k in order:
        other = partner(me, k)
        span = slice(None) if k == 1 else columns
        copies[k] = pltpu.make_async_remote_copy(
            src_ref=src.at[rows(other), span],
            dst_ref=out.at[rows(me), span],
            send_sem=send1.at[k],
            recv_sem=recv1.at[k],
            device_id=(other, tile),
            device_id_type=MESH,
        )
        copies[k].start()
    for k in order:
        copies[k].wait_recv()
        if k == 1:
            continue
        block = out.at[rows(partner(me, k)), columns]
        for m in range(1, tiles):
            pltpu.make_async_remote_copy(
                src_ref=block,
                dst_ref=block,
                send_sem=send2.at[m],
                recv_sem=recv2.at[m],
                device_id=(me, (tile + m) % tiles),
                device_id_type=MESH,
            ).start()
    for k in order:
        copies[k].wait_send()
    own.wait()
    passed = out.at[pl.ds(0, (len(order) - 1) * cap), columns]
    for m in range(1, tiles):
        pltpu.make_async_copy(passed, passed, send2.at[m]).wait()
        pltpu.make_async_copy(passed, passed, recv2.at[m]).wait()


def return_kernel(
    sessions,
    tiles,
    cap,
    answer,
    mix_hi,
    mix_lo,
    tokens,
    gain,
    w_proj,
    out,
    stage,
    reduced,
    back,
    mine,
    theirs,
    send_a,
    recv_a,
    send_b,
    recv_b,
    send_c,
    recv_c,
):
    me, tile = lax.axis_index("sess"), lax.axis_index("exp")
    width = answer.shape[1]
    part = width // tiles
    channels = w_proj.shape[1]

    def rows(index):
        return pl.ds(pl.multiple_of(index * cap, cap), cap)

    def columns(index, offset=0, size=part):
        return pl.ds(pl.multiple_of(index * part + offset, 128), size)

    enter(me, tile, sessions, tiles)
    order = exchange_order(sessions)
    order = [k for k in order if k >= 4] + [k for k in order if k < 4] + [0]
    arrivals = {}
    for k in order:
        other = partner(me, k)
        for m in range(1, tiles):
            peer = (tile + m) % tiles
            arrivals[m, k] = pltpu.make_async_remote_copy(
                src_ref=answer.at[rows(other), columns(peer)],
                dst_ref=stage.at[m - 1, rows(other), :],
                send_sem=send_a.at[m],
                recv_sem=recv_a.at[m, k],
                device_id=(me, peer),
                device_id_type=MESH,
            )
            arrivals[m, k].start()
    returns = {}
    for k in order:
        other = partner(me, k)
        total = answer[rows(other), columns(tile)].astype(jnp.float32)
        for m in range(1, tiles):
            arrivals[m, k].wait_recv()
            total = total + stage[m - 1, rows(other), :].astype(jnp.float32)
        if k == 0:
            back[rows(me), :] = total.astype(jnp.bfloat16)
            continue
        reduced[rows(other), :] = total.astype(jnp.bfloat16)
        returns[k] = pltpu.make_async_remote_copy(
            src_ref=reduced.at[rows(other), :],
            dst_ref=back.at[rows(me), :],
            send_sem=send_b.at[k],
            recv_sem=recv_b.at[k],
            device_id=(other, tile),
            device_id_type=MESH,
        )
        returns[k].start()
    for k in order[:-1]:
        returns[k].wait_recv()
    step = min(512, part)
    square = jnp.zeros((tokens.shape[0], 1), jnp.float32)
    coarse = jnp.zeros((tokens.shape[0], channels), jnp.float32)
    for begin in range(0, part, step):
        block = back[:, begin : begin + step]
        mixed = jnp.dot(mix_hi[...], block, preferred_element_type=jnp.float32) + jnp.dot(
            mix_lo[...], block, preferred_element_type=jnp.float32
        )
        span = columns(tile, begin, step)
        feat = (tokens[:, span].astype(jnp.float32) + mixed).astype(jnp.bfloat16)
        feat = feat.astype(jnp.float32)
        square = square + jnp.sum(feat * feat, axis=1, keepdims=True)
        scaled = (feat * gain[:, span]).astype(jnp.bfloat16)
        coarse = coarse + jnp.dot(scaled, w_proj[span, :], preferred_element_type=jnp.float32)
    mine[:, :channels] = coarse
    mine[:, channels:] = jnp.broadcast_to(square, (tokens.shape[0], 128))
    sums = []
    for m in range(1, tiles):
        sums.append(
            pltpu.make_async_remote_copy(
                src_ref=mine,
                dst_ref=theirs.at[m - 1],
                send_sem=send_c.at[m],
                recv_sem=recv_c.at[m],
                device_id=(me, (tile + m) % tiles),
                device_id_type=MESH,
            )
        )
        sums[-1].start()
    for m, copy in enumerate(sums):
        copy.wait_recv()
        coarse = coarse + theirs[m, :, :channels]
        square = square + theirs[m, :, channels : channels + 1]
    out[...] = (coarse * lax.rsqrt(square * (1.0 / width) + epsilon)).astype(jnp.bfloat16)
    for copy in sums:
        copy.wait_send()
    for k in order[:-1]:
        returns[k].wait_send()
    for m in range(1, tiles):
        sent = stage.at[m - 1]
        pltpu.make_async_copy(sent, sent, send_a.at[m]).wait()


def dispatch(outgoing, sessions, tiles, cap):
    return pl.pallas_call(
        functools.partial(dispatch_kernel, sessions, tiles, cap),
        out_shape=jax.ShapeDtypeStruct(outgoing.shape, outgoing.dtype),
        in_specs=[VMEM],
        out_specs=VMEM,
        scratch_shapes=[
            pltpu.SemaphoreType.DMA,
            pltpu.SemaphoreType.DMA((sessions,)),
            pltpu.SemaphoreType.DMA((sessions,)),
            pltpu.SemaphoreType.DMA((tiles,)),
            pltpu.SemaphoreType.DMA((tiles,)),
        ],
        compiler_params=pltpu.CompilerParams(
            collective_id=0, has_side_effects=True, vmem_limit_bytes=30 * 2**20
        ),
        name="dispatch",
    )(outgoing)


def bring_back(answer, mix_hi, mix_lo, tokens, gain, w_proj, sessions, tiles, cap):
    slots, width = answer.shape
    part = width // tiles
    count, channels = tokens.shape[0], w_proj.shape[1]
    return pl.pallas_call(
        functools.partial(return_kernel, sessions, tiles, cap),
        out_shape=jax.ShapeDtypeStruct((count, channels), jnp.bfloat16),
        in_specs=[VMEM] * 6,
        out_specs=VMEM,
        scratch_shapes=[
            pltpu.VMEM((tiles - 1, slots, part), jnp.bfloat16),
            pltpu.VMEM((slots, part), jnp.bfloat16),
            pltpu.VMEM((slots, part), jnp.bfloat16),
            pltpu.VMEM((count, channels + 128), jnp.float32),
            pltpu.VMEM((tiles - 1, count, channels + 128), jnp.float32),
            pltpu.SemaphoreType.DMA((tiles,)),
            pltpu.SemaphoreType.DMA((tiles, sessions)),
            pltpu.SemaphoreType.DMA((sessions,)),
            pltpu.SemaphoreType.DMA((sessions,)),
            pltpu.SemaphoreType.DMA((tiles,)),
            pltpu.SemaphoreType.DMA((tiles,)),
        ],
        compiler_params=pltpu.CompilerParams(
            collective_id=1, has_side_effects=True, vmem_limit_bytes=45 * 2**20
        ),
        name="bring_back",
    )(answer, mix_hi, mix_lo, tokens, gain, w_proj)


def extended(cells, axis, dim, width):
    count = lax.axis_size(axis)
    ends = count - 1
    head = lax.slice_in_dim(cells, 0, width, axis=dim)
    tail = lax.slice_in_dim(cells, cells.shape[dim] - width, cells.shape[dim], axis=dim)
    return jnp.concatenate(
        [
            lax.ppermute(tail, axis, [(i, i + 1) for i in range(ends)]),
            cells,
            lax.ppermute(head, axis, [(i + 1, i) for i in range(ends)]),
        ],
        axis=dim,
    )


def slot_targets(routes, capacity):
    flat = routes.reshape(-1)
    place = jnp.arange(flat.shape[0], dtype=jnp.int32)
    earlier = (flat[:, None] == flat[None, :]) & (place[None, :] < place[:, None])
    return flat * capacity + jnp.sum(earlier.astype(jnp.int32), axis=1)


def patches(frames, height):
    breadth = frames.shape[2]
    padded = jnp.pad(frames, ((0, 0), (0, 0), (1, 1), (0, 0)))
    pieces = [
        padded[t, dy : dy + height, dx : dx + breadth, :]
        for t in range(frames.shape[0])
        for dy in range(3)
        for dx in range(3)
    ]
    return jnp.concatenate(pieces, axis=-1).reshape(height * breadth, -1)


def body(
    tokens,
    routes,
    gates,
    w_gate,
    w_up,
    w_down,
    feat_gain,
    w_proj,
    conv_time,
    bias_time,
    conv_space,
    bias_space,
    frame_cache,
    cache_head,
):
    sessions, tiles = lax.axis_size("sess"), lax.axis_size("exp")
    tile = lax.axis_index("exp")
    channels = w_proj.shape[-1]
    local = tokens[0]
    tok_count = local.shape[0]
    cap = 2 * tok_count * TOPK // sessions
    height, breadth = frame_cache.shape[2:4]
    rows_own = tok_count // tiles

    head = cache_head[0]
    cache = frame_cache[:, 0]
    past = jnp.stack(
        [
            lax.dynamic_index_in_dim(cache, (head + 2) % 3, 0, keepdims=False),
            lax.dynamic_index_in_dim(cache, head, 0, keepdims=False),
        ]
    )
    past = extended(past, "exp", 1, HALO)

    dest = slot_targets(routes[0], cap).reshape(tok_count, TOPK)
    slots = jnp.arange(sessions * cap, dtype=jnp.int32)
    hit = dest[:, :, None] == slots[None, None, :]
    onehot = jnp.any(hit, axis=1).astype(jnp.bfloat16)
    weight = jnp.sum(jnp.where(hit, gates[0][:, :, None], 0.0), axis=1)
    mix_hi = lax.reduce_precision(weight, 8, 7)
    mix_lo = (weight - mix_hi).astype(jnp.bfloat16)
    mix_hi = mix_hi.astype(jnp.bfloat16)
    outgoing = lax.dot_general(
        onehot, local, (((0,), (0,)), ((), ())), preferred_element_type=jnp.float32
    ).astype(jnp.bfloat16)

    rows = dispatch(outgoing, sessions, tiles, cap)
    gate = jnp.dot(rows, w_gate[0], preferred_element_type=jnp.float32)
    upward = jnp.dot(rows, w_up[0], preferred_element_type=jnp.float32)
    hidden = (jax.nn.silu(gate) * upward).astype(jnp.bfloat16)
    answer = jnp.dot(hidden, w_down[0], preferred_element_type=jnp.float32).astype(jnp.bfloat16)
    coarse = bring_back(
        answer, mix_hi, mix_lo, local, feat_gain[None, :], w_proj, sessions, tiles, cap
    )

    coarse = jnp.pad(coarse, ((GRID_W, GRID_W), (0, 0)))
    coarse = lax.dynamic_slice_in_dim(coarse, tile * rows_own, rows_own + 2 * GRID_W, 0)
    coarse = coarse.reshape(-1, GRID_W, channels)
    fine = jnp.repeat(jnp.repeat(coarse, 2, axis=0), 2, axis=1)
    stack = jnp.concatenate([past, fine[None]], axis=0)
    first = jnp.dot(
        patches(stack, height + 2),
        conv_time.reshape(-1, channels),
        preferred_element_type=jnp.float32,
    )
    active = jax.nn.silu(first + bias_time).astype(jnp.bfloat16)
    active = active.reshape(height + 2, breadth, channels)
    row = tile * height - 1 + jnp.arange(height + 2, dtype=jnp.int32)
    inside = (row >= 0) & (row < height * tiles)
    active = jnp.where(inside[:, None, None], active, jnp.zeros_like(active))
    second = jnp.dot(
        patches(active[None], height),
        conv_space.reshape(-1, channels),
        preferred_element_type=jnp.float32,
    )
    own = fine[HALO : HALO + height].reshape(-1, channels)
    result = own.astype(jnp.float32) + second + bias_space
    return result.astype(jnp.bfloat16).reshape(1, height, breadth, channels)


def solution(mesh):
    return jax.shard_map(
        body,
        mesh=mesh,
        in_specs=(
            P("sess", None, None),
            P("sess", None, None),
            P("sess", None, None),
            P("sess", None, "exp"),
            P("sess", None, "exp"),
            P("sess", "exp", None),
            P(),
            P(),
            P(),
            P(),
            P(),
            P(),
            P(None, "sess", "exp", None, None),
            P("sess"),
        ),
        out_specs=P("sess", "exp", None, None),
        check_vma=False,
    )
```

time: 215 us -> 134 us (0.62)
  Pallas kernels: 0 us -> 74.3 us
  waiting for transfers between devices: 65.8 us -> 0.01 us
  blocking collectives: 54.5 us -> 0 us
  between operations: 14.5 us -> 1.4 us
  other arithmetic: 16.3 us -> 6.55 us
  local copies, waits for them, and re-layouts: 27.7 us -> 21.8 us
  starting transfers between devices: 12.4 us -> 6.77 us
    pallas_call x0 -> x2, Pallas kernels: none -> 74.3 us  [the longest x1 38.8 us: dispatch(): pl.pallas_call(functools.partial(dispatch_kernel, sessions, tiles, cap),...]
    all_to_all x1 -> x0, blocking collectives: 54.5 us -> none  [body(): lax.all_to_all(outgoing, 'sess', split_axis=0, concat_axis=0, tiled=True)]
    all_to_all x1 -> x0, waiting for transfers between devices: 40.3 us -> none  [body(): lax.all_to_all(answer, 'sess', split_axis=0, concat_axis=0, tiled=True)]
    reduce_scatter x1 -> x0, waiting for transfers between devices: 18.9 us -> none  [body(): lax.psum_scatter(combined.astype(jnp.bfloat16), 'exp', scatter_dimension=...]
    reduce_sum x4 -> x2, other arithmetic: 9.54 us -> 0.27 us  [the longest x1 0.18 us: slot_targets(): return flat * capacity + jnp.sum(earlier.astype(jnp.int32), axis=1)]
    scatter x1 -> x0, local copies, waits for them, and re-layouts: 6.98 us -> none  [body(): jnp.zeros((sess_count * capacity, width), jnp.bfloat16).at[dest]]
    unnamed x51 -> x77, local copies, waits for them, and re-layouts: 3.97 us -> 10.9 us
    ppermute x4 -> x2, waiting for transfers between devices: 6.63 us -> 0.01 us  [the longest x1 0.01 us: extended(): lax.ppermute(tail, axis, [(i, i + 1) for i in range(ends)])]
  transfers between devices with their start and end apart: 6 -> 2, of which waited for: 5 -> 0; matrix products, arithmetic and copies ran while one was open for 2% -> 26% of each run, Pallas kernels for 0% -> 56%
where the time goes in v1:
time: 134 us; the launch traced here: 133 us
  Pallas kernels  74.3 us (55%)
  matrix products  22.2 us (17%)
  local copies, waits for them, and re-layouts  21.8 us (16%)
  starting transfers between devices  6.77 us (5%)
  other arithmetic  6.55 us (5%)
  between operations  1.4 us (1%)
    pallas_call x1, Pallas kernels, dispatch(): pl.pallas_call(functools.partial(dispatch_kernel, sessions, tiles, cap),...  38.8 us
    pallas_call x1, Pallas kernels, bring_back(): pl.pallas_call(functools.partial(return_kernel, sessions, tiles, cap), ou...  35.4 us
    dot_general x1, matrix products, body(): jnp.dot(hidden, w_down[0], preferred_element_type=jnp.float32)  12.8 us
    unnamed x77, local copies, waits for them, and re-layouts  10.9 us
    dot_general x1, matrix products, body(): gate = jnp.dot(rows, w_gate[0], preferred_element_type=jnp.float32)  5.84 us
    ppermute x1, starting transfers between devices, extended(): lax.ppermute(tail, axis, [(i, i + 1) for i in range(ends)])  5.49 us
  transfers between devices with their start and end apart: 2, of which 0 were waited for; matrix products, arithmetic and copies ran while one was open for 26% of the time, Pallas kernels for 56%

profile of v1, /device:TPU:0, one launch (start us, length us, event | category | flops | bytes accessed | tf_op | source)
XLA Modules:
  0.0 133.0 jit_solution(14743670228719365239)
XLA Ops:
  0.0 0.0 copy-start
  0.8 1.1 dynamic-slice_bitcast_fusion.1
  1.9 0.0 copy-start.9
  1.9 0.0 copy-start.11
  1.9 0.6 copy-done.9
  2.5 0.6 pad_maximum_fusion.6
  3.1 0.0 copy-done.11
  3.1 5.5 %collective-permute-start = (bf16[2,2,16,256]{3,2,1,0:T(8,128)(2,1)}, bf16[2,2,16,256]{3,2,1,0:T(8,128)(2,1)}, u32[]{:S(2)}, u32[]{:S(2)}) collective-permute-start(bf16[2,2,16,256]{3,2,1,0:T(8,128)(2,1)} %get-tuple-element.33), channel_id=1, source_target_pairs={{0,1},{2,3},{4,5},{6,7},{8,9},{10,11},{12,13},{14,15},{16,17},{18,... | collective-permute-start | bytes 98312 | tf_op jit(solution)/shard_map/ppermute | solution.py:270
  8.6 1.3 collective-permute-start.1
  9.9 1.4 %copy.23 = s32[1,64,2]{2,1,0:T(8,128)} copy(s32[1,64,2]{1,2,0:T(2,128)} %param.15) | data formatting | bytes 1024 | tf_op args[1]
  11.3 0.9 eq.30
  12.2 0.2 convert_reduce_fusion
  12.4 0.8 reduce_sum.21
  13.1 0.8 copy.24
  13.9 0.7 bitcast_add_fusion
  14.6 0.1 fusion.24
  14.7 1.8 %convolution_convert_fusion.src = bf16[256,4096]{1,0:T(8,128)(2,1)S(1)} fusion(pred[64,256]{1,0:T(8,128)(4,1)S(1)} %fusion.24, bf16[1,64,4096]{2,1,0:T(8,128)(2,1)} %param.14), kind=kOutput, calls=%fused_computation.7 | convolution fusion | flops 135266304 | bytes 2637824 | tf_op jit(solution)/shard_map/dot_general | solution.py:340
  16.5 0.0 copy-start.19
  16.5 38.8 %dispatch.1 = bf16[256,4096]{1,0:T(8,128)(2,1)S(1)} custom-call(bf16[256,4096]{1,0:T(8,128)(2,1)S(1)} %convolution_convert_fusion.src), custom_call_target="tpu_custom_call" | custom-call | tf_op jit(solution)/shard_map/dispatch/pallas_call | solution.py:215
  55.4 0.0 copy-start.4
  55.4 1.3 copy-done.4
  56.7 0.0 copy-done.19
  56.7 0.1 select_reduce_fusion
  56.8 0.6 fusion.25
  57.4 5.8 %fusion.4 = f32[256,704]{0,1:T(8,128)} fusion(bf16[256,4096]{1,0:T(8,128)(2,1)} %copy-done.4, bf16[1,4096,704]{1,2,0:T(8,128)(2,1)} %param.17), kind=kOutput, calls=%fused_computation.4 | convolution fusion | flops 1476395008 | bytes 8585216 | tf_op jit(solution)/shard_map/dot_general | solution.py:345
  63.3 12.8 %fusion.6.answer = bf16[256,4096]{1,0:T(8,128)(2,1)} fusion(bf16[1,704,4096]{2,1,0:T(8,128)(2,1)} %param.19, bf16[256,4096]{1,0:T(8,128)(2,1)} %copy-done.4, bf16[1,4096,704]{1,2,0:T(8,128)(2,1)} %param.18, f32[256,704]{0,1:T(8,128)} %fusion.4), kind=kOutput, calls=%fused_computation.6 | convolution fusion | flops 2954919936 | bytes 16449536 | tf_op jit(solution)/shard_map/dot_general | solution.py:348
  76.1 0.0 copy-done.8
  76.1 1.0 copy-done.1
  77.1 1.6 %copy-done.2 = bf16[4096,256]{1,0:T(8,128)(2,1)S(1)} copy-done((bf16[4096,256]{1,0:T(8,128)(2,1)S(1)}, bf16[4096,256]{1,0:T(8,128)(2,1)}, u32[]{:S(2)}) %copy-start.2) | copy-done | bytes 2097176
  78.7 1.6 %copy-done.3 = bf16[256,4096]{1,0:T(8,128)(2,1)S(1)} copy-done((bf16[256,4096]{1,0:T(8,128)(2,1)S(1)}, bf16[256,4096]{1,0:T(8,128)(2,1)}, u32[]{:S(2)}) %copy-start.3) | copy-done | bytes 2097176
  80.3 0.8 copy-done.6
  81.1 0.8 copy-done.7
  81.8 35.4 %bring_back.1 = bf16[64,256]{1,0:T(8,128)(2,1)S(1)} custom-call(bf16[256,4096]{1,0:T(8,128)(2,1)S(1)} %copy-done.3, bf16[64,256]{1,0:T(8,128)(2,1)S(1)} %copy-done.7, bf16[64,256]{1,0:T(8,128)(2,1)S(1)} %copy-done.6, bf16[64,4096]{1,0:T(8,128)(2,1)S(1)} %bitcast.90, f32[1,4096]{1,0:T(1,128)S(1)} %bitcast.91, bf16[4096,256]{1,0:T(8,128)(2,1)S(1)} %copy-done.2), custom_call_target="tpu_custom_call" | custom-call | tf_op jit(solution)/shard_map/bring_back/pallas_call | solution.py:238
  117.3 0.0 copy-start.5
  117.3 0.6 copy-done.5
  117.9 0.7 broadcast_in_dim.53
  118.6 1.6 %broadcast_in_dim_reshape.4 = bf16[1,12,16,256]{3,2,1,0:T(8,128)(2,1)} reshape(bf16[12,8,2,256]{3,2,1,0:T(2,128)(2,1)} %broadcast_in_dim.53) | data formatting | bytes 196608 | tf_op jit(solution)/shard_map/broadcast_in_dim;reshape | solution.py:357
  120.2 1.7 %fusion.35 = (bf16[1,10,16,256]{3,2,1,0:T(8,128)(2,1)}, bf16[1,10,16,256]{3,2,1,0:T(8,128)(2,1)}, bf16[1,10,16,256]{3,2,1,0:T(8,128)(2,1)}) fusion(bf16[1,12,16,256]{3,2,1,0:T(8,128)(2,1)} %broadcast_in_dim_reshape.4), kind=kLoop, calls=%fused_computation.99 | loop fusion | bytes 491520 | tf_op jit(solution)/shard_map/slice | solution.py:289
  121.9 1.3 fusion.29
  123.2 0.8 broadcast_in_dim.49
  124.0 0.7 broadcast_in_dim.50
  124.7 1.6 %convert_element_type.54 = f32[128,256]{1,0:T(8,128)} reshape(f32[8,8,2,256]{3,2,1,0:T(2,128)} %broadcast_in_dim.50) | data formatting | bytes 262144 | tf_op jit(solution)/shard_map/convert_element_type | solution.py:374
  126.3 0.0 collective-permute-done
  126.3 0.0 collective-permute-done.1
  126.4 1.2 select_maximum_fusion
  127.6 0.2 fusion.32
  127.7 0.0 copy-done.10
  127.8 0.0 copy-done.12
  127.8 0.0 copy-start.17
  127.8 0.8 pad_maximum_fusion
  128.7 0.0 copy-start.20
  128.7 0.8 pad_maximum_fusion.1
  129.8 0.0 copy-done.17
  129.9 0.0 copy-done.15
  129.9 0.0 copy-done
  129.9 0.0 copy-done.20
  129.9 0.8 multiply_convert_fusion
  130.7 0.0 copy-start.13
  130.7 0.0 copy-start.14
  130.7 0.0 copy-start.18
  130.8 0.1 broadcast_select_fusion
  131.0 1.0 copy-done.13
  132.0 0.0 copy-done.18
  132.0 1.0 fusion.16
  (53 shorter events, 0.4 us)
Async XLA Ops:
  0.0 129.9 %copy-start = (bf16[3,3,3,256,256]{4,3,2,1,0:T(8,128)(2,1)S(1)}, bf16[3,3,3,256,256]{4,3,2,1,0:T(8,128)(2,1)}, u32[]{:S(2)}) copy-start(bf16[3,3,3,256,256]{4,3,2,1,0:T(8,128)(2,1)} %param.22) | copy-start | bytes 10616836
  1.9 0.6 copy-start.9
  1.9 1.2 copy-start.11
  3.1 123.2 %collective-permute-start = (bf16[2,2,16,256]{3,2,1,0:T(8,128)(2,1)}, bf16[2,2,16,256]{3,2,1,0:T(8,128)(2,1)}, u32[]{:S(2)}, u32[]{:S(2)}) collective-permute-start(bf16[2,2,16,256]{3,2,1,0:T(8,128)(2,1)} %get-tuple-element.33), channel_id=1, source_target_pairs={{0,1},{2,3},{4,5},{6,7},{8,9},{10,11},{12,13},{14,15},{16,17},{18,... | collective-permute-start | bytes 98312 | tf_op jit(solution)/shard_map/ppermute | solution.py:270
  8.6 117.7 %collective-permute-start.1 = (bf16[2,2,16,256]{3,2,1,0:T(8,128)(2,1)}, bf16[2,2,16,256]{3,2,1,0:T(8,128)(2,1)}, u32[]{:S(2)}, u32[]{:S(2)}) collective-permute-start(bf16[2,2,16,256]{3,2,1,0:T(8,128)(2,1)} %get-tuple-element.34), channel_id=1, source_target_pairs={{1,0},{3,2},{5,4},{7,6},{9,8},{11,10},{13,12},{15,14},{17,16},{19,... | collective-permute-start | bytes 98312 | tf_op jit(solution)/shard_map/ppermute | solution.py:272
  16.5 40.2 %copy-start.19 = (f32[1,64,2]{1,2,0:T(2,128)S(1)}, f32[1,64,2]{1,2,0:T(2,128)}, u32[]{:S(2)}) copy-start(f32[1,64,2]{1,2,0:T(2,128)} %param.16) | copy-start | bytes 1540
  55.4 1.3 copy-start.4
  63.3 12.8 %copy-start.8 = (f32[4096]{0:T(1024)S(1)}, f32[4096]{0:T(1024)}, u32[]{:S(2)}) copy-start(f32[4096]{0:T(1024)} %param.20) | copy-start | bytes 49156
  76.1 1.0 copy-start.1
  77.1 1.6 %copy-start.2 = (bf16[4096,256]{1,0:T(8,128)(2,1)S(1)}, bf16[4096,256]{1,0:T(8,128)(2,1)}, u32[]{:S(2)}) copy-start(bf16[4096,256]{1,0:T(8,128)(2,1)} %w_proj.1) | copy-start | bytes 6291460
  78.7 1.6 %copy-start.3 = (bf16[256,4096]{1,0:T(8,128)(2,1)S(1)}, bf16[256,4096]{1,0:T(8,128)(2,1)}, u32[]{:S(2)}) copy-start(bf16[256,4096]{1,0:T(8,128)(2,1)} %fusion.6.answer) | copy-start | bytes 6291460
  80.3 0.8 copy-start.6
  81.1 0.8 copy-start.7
  117.3 0.6 copy-start.5
  126.3 1.4 %copy-start.10 = (bf16[1,8,16,256]{3,2,1,0:T(8,128)(2,1)S(1)}, bf16[1,8,16,256]{3,2,1,0:T(8,128)(2,1)}, u32[]{:S(2)}) copy-start(bf16[1,8,16,256]{3,2,1,0:T(8,128)(2,1)} %copy-done.9) | copy-start | bytes 196612
  126.3 1.4 %copy-start.12 = (bf16[1,8,16,256]{3,2,1,0:T(8,128)(2,1)S(1)}, bf16[1,8,16,256]{3,2,1,0:T(8,128)(2,1)}, u32[]{:S(2)}) copy-start(bf16[1,8,16,256]{3,2,1,0:T(8,128)(2,1)} %copy-done.11) | copy-start | bytes 196612
  127.8 2.0 %copy-start.17 = (bf16[1,10,16,256]{3,2,1,0:T(8,128)(2,1)S(1)}, bf16[1,10,16,256]{3,2,1,0:T(8,128)(2,1)}, u32[]{:S(2)}) copy-start(bf16[1,10,16,256]{3,2,1,0:T(8,128)(2,1)} %get-tuple-element.37) | copy-start | bytes 245764
  128.6 1.2 copy-start.16
  128.7 1.2 copy-start.15
  128.7 1.2 copy-start.20
  130.7 1.3 copy-start.13
  130.7 1.3 copy-start.14
  130.7 1.3 copy-start.18

commit v2 on v1

--- a/solution.py
+++ b/solution.py
@@ -46,7 +46,43 @@
     pl.semaphore_wait(barrier, sessions - 1 + tiles - 1)
 
 
-def dispatch_kernel(sessions, tiles, cap, src, out, own_sem, send1, recv1, send2, recv2):
+def silu(value):
+    return value / (1.0 + jnp.exp(-value))
+
+
+def across(left, right):
+    return lax.dot_general(
+        left, right, (((1,), (1,)), ((), ())), preferred_element_type=jnp.float32
+    )
+
+
+def dispatch_kernel(
+    sessions,
+    tiles,
+    cap,
+    src,
+    past,
+    w_gate,
+    w_up,
+    w_down,
+    answer,
+    halo,
+    out,
+    gate_w,
+    up_w,
+    down_w,
+    gate,
+    upward,
+    hidden,
+    own_sem,
+    load_sem,
+    halo_send,
+    halo_recv,
+    send1,
+    recv1,
+    send2,
+    recv2,
+):
     me, tile = lax.axis_index("sess"), lax.axis_index("exp")
     width = src.shape[1]
     part = width // tiles
@@ -55,6 +91,14 @@
     def rows(index):
         return pl.ds(pl.multiple_of(index * cap, cap), cap)
 
+    loads = [
+        pltpu.make_async_copy(source, held, load_sem.at[i])
+        for i, (source, held) in enumerate(
+            ((w_gate, gate_w), (w_up, up_w), (w_down, down_w))
+        )
+    ]
+    for load in loads:
+        load.start()
     enter(me, tile, sessions, tiles)
     own = pltpu.make_async_copy(src.at[rows(me), :], out.at[rows(me), :], own_sem)
     own.start()
@@ -72,6 +116,20 @@
             device_id_type=MESH,
         )
         copies[k].start()
+    height = past.shape[1]
+    borders = []
+    for side, begin, step in ((0, height - HALO, 1), (1, 0, tiles - 1)):
+        borders.append(
+            pltpu.make_async_remote_copy(
+                src_ref=past.at[:, begin : begin + HALO],
+                dst_ref=halo.at[side],
+                send_sem=halo_send.at[side],
+                recv_sem=halo_recv.at[side],
+                device_id=(me, (tile + step) % tiles),
+                device_id_type=MESH,
+            )
+        )
+        borders[-1].start()
     for k in order:
         copies[k].wait_recv()
         if k == 1:
@@ -93,6 +151,30 @@
     for m in range(1, tiles):
         pltpu.make_async_copy(passed, passed, send2.at[m]).wait()
         pltpu.make_async_copy(passed, passed, recv2.at[m]).wait()
+    for copy in borders:
+        copy.wait()
+    for load in loads:
+        load.wait()
+    depth = width // 4
+    gate[...] = jnp.zeros_like(gate)
+    upward[...] = jnp.zeros_like(upward)
+
+    @pl.loop(0, width // depth)
+    def _(step):
+        span = pl.ds(pl.multiple_of(step * depth, depth), depth)
+        block = out[:, span]
+        gate[...] += across(block, gate_w[:, span])
+        upward[...] += across(block, up_w[:, span])
+
+    hidden[...] = (silu(gate[...]) * upward[...]).astype(jnp.bfloat16)
+    piece = width // 8
+
+    @pl.loop(0, width // piece)
+    def _(step):
+        span = pl.ds(pl.multiple_of(step * piece, piece), piece)
+        answer[:, span] = jnp.dot(
+            hidden[...], down_w[:, span], preferred_element_type=jnp.float32
+        ).astype(jnp.bfloat16)
 
 
 def return_kernel(
@@ -102,10 +184,13 @@
     answer,
     mix_hi,
     mix_lo,
+    all_tokens,
+    gain,
+    all_proj,
+    out,
     tokens,
-    gain,
     w_proj,
-    out,
+    load_sem,
     stage,
     reduced,
     back,
@@ -129,6 +214,12 @@
     def columns(index, offset=0, size=part):
         return pl.ds(pl.multiple_of(index * part + offset, 128), size)
 
+    loads = [
+        pltpu.make_async_copy(all_tokens.at[:, columns(tile)], tokens, load_sem.at[0]),
+        pltpu.make_async_copy(all_proj.at[columns(tile), :], w_proj, load_sem.at[1]),
+    ]
+    for load in loads:
+        load.start()
     enter(me, tile, sessions, tiles)
     order = exchange_order(sessions)
     order = [k for k in order if k >= 4] + [k for k in order if k < 4] + [0]
@@ -168,6 +259,8 @@
         returns[k].start()
     for k in order[:-1]:
         returns[k].wait_recv()
+    for load in loads:
+        load.wait()
     step = min(512, part)
     square = jnp.zeros((tokens.shape[0], 1), jnp.float32)
     coarse = jnp.zeros((tokens.shape[0], channels), jnp.float32)
@@ -177,11 +270,12 @@
             mix_lo[...], block, preferred_element_type=jnp.float32
         )
         span = columns(tile, begin, step)
-        feat = (tokens[:, span].astype(jnp.float32) + mixed).astype(jnp.bfloat16)
+        here = slice(begin, begin + step)
+        feat = (tokens[:, here].astype(jnp.float32) + mixed).astype(jnp.bfloat16)
         feat = feat.astype(jnp.float32)
         square = square + jnp.sum(feat * feat, axis=1, keepdims=True)
         scaled = (feat * gain[:, span]).astype(jnp.bfloat16)
-        coarse = coarse + jnp.dot(scaled, w_proj[span, :], preferred_element_type=jnp.float32)
+        coarse = coarse + jnp.dot(scaled, w_proj[here, :], preferred_element_type=jnp.float32)
     mine[:, :channels] = coarse
     mine[:, channels:] = jnp.broadcast_to(square, (tokens.shape[0], 128))
     sums = []
@@ -201,7 +295,9 @@
         copy.wait_recv()
         coarse = coarse + theirs[m, :, :channels]
         square = square + theirs[m, :, channels : channels + 1]
-    out[...] = (coarse * lax.rsqrt(square * (1.0 / width) + epsilon)).astype(jnp.bfloat16)
+    out[...] = (coarse * lax.rsqrt(square * (1.0 / width) + epsilon)).astype(jnp.bfloat16).astype(
+        jnp.float32
+    )
     for copy in sums:
         copy.wait_send()
     for k in order[:-1]:
@@ -211,24 +307,207 @@
         pltpu.make_async_copy(sent, sent, send_a.at[m]).wait()
 
 
-def dispatch(outgoing, sessions, tiles, cap):
+def route_kernel(
+    sessions, cap, routes, gates, tokens, head, cache, outgoing, mix_hi, mix_lo, past
+):
+    count = tokens.shape[0]
+    slots = sessions * cap
+    past[1] = cache[head[0]]
+    past[0] = cache[lax.rem(head[0] + 2, 3)]
+    expert = lax.broadcasted_iota(jnp.int32, (sessions, count), 0)
+    named = [(routes[k : k + 1, :] == expert).astype(jnp.float32) for k in range(TOPK)]
+    earlier = lax.broadcasted_iota(jnp.int32, (count, count), 0) < lax.broadcasted_iota(
+        jnp.int32, (count, count), 1
+    )
+    before = jnp.dot(
+        sum(named).astype(jnp.bfloat16),
+        earlier.astype(jnp.float32).astype(jnp.bfloat16),
+        preferred_element_type=jnp.float32,
+    )
+    slot = lax.broadcasted_iota(jnp.int32, (slots, count), 0)
+    onehot = jnp.zeros((slots, count), jnp.float32)
+    weight = jnp.zeros((slots, count), jnp.float32)
+    for k in range(TOPK):
+        place = jnp.sum(before * named[k], axis=0, keepdims=True).astype(jnp.int32)
+        hit = slot == routes[k : k + 1, :] * cap + place
+        onehot = onehot + jnp.where(hit, 1.0, 0.0)
+        weight = weight + jnp.where(hit, gates[k : k + 1, :], 0.0)
+        before = before + named[k]
+    weight = weight.T
+    high = weight.astype(jnp.bfloat16)
+    mix_hi[...] = high
+    mix_lo[...] = (weight - high.astype(jnp.float32)).astype(jnp.bfloat16)
+    onehot = onehot.astype(jnp.bfloat16)
+    step = 512
+    for begin in range(0, tokens.shape[1], step):
+        outgoing[:, begin : begin + step] = jnp.dot(
+            onehot, tokens[:, begin : begin + step], preferred_element_type=jnp.float32
+        ).astype(jnp.bfloat16)
+
+
+def route(routes, gates, tokens, head, cache, sessions, cap):
+    slots, count = sessions * cap, tokens.shape[0]
+    mix = jax.ShapeDtypeStruct((count, slots), jnp.bfloat16)
+    return pl.pallas_call(
+        functools.partial(route_kernel, sessions, cap),
+        out_shape=(
+            jax.ShapeDtypeStruct((slots, tokens.shape[1]), jnp.bfloat16),
+            mix,
+            mix,
+            jax.ShapeDtypeStruct((2,) + cache.shape[1:], cache.dtype),
+        ),
+        in_specs=[VMEM, VMEM, VMEM, pl.BlockSpec(memory_space=pltpu.SMEM), VMEM],
+        out_specs=(VMEM,) * 4,
+        compiler_params=pltpu.CompilerParams(vmem_limit_bytes=30 * 2**20),
+        name="route",
+    )(routes, gates, tokens, head, cache)
+
+
+def conv_kernel(
+    coarse,
+    past,
+    halo,
+    w_time,
+    bias_time,
+    w_space,
+    bias_space,
+    out,
+    above,
+    frames,
+    wide,
+    wide_active,
+):
+    tile, tiles = lax.axis_index("exp"), lax.axis_size("exp")
+    tall, channels = frames.shape[1:]
+    breadth = 2 * GRID_W
+    edge = HALO * breadth
+    count = out.shape[0]
+    grid_rows = coarse.shape[0] // GRID_W
+    own_rows = grid_rows // tiles
+
+    for r in range(own_rows + 2):
+        row = tile * own_rows - 1 + r
+        at = jnp.clip(row, 0, grid_rows - 1)
+        value = coarse[pl.ds(pl.multiple_of(at * GRID_W, GRID_W), GRID_W), :]
+        above[r * GRID_W : (r + 1) * GRID_W, :] = jnp.where(
+            (row >= 0) & (row < grid_rows), value, jnp.zeros_like(value)
+        )
+    for t in range(2):
+        top, bottom = halo[0, t], halo[1, t]
+        frames[t, :edge, :] = jnp.where(tile > 0, top, jnp.zeros_like(top))
+        frames[t, edge : edge + count, :] = past[t]
+        frames[t, edge + count :, :] = jnp.where(
+            tile < tiles - 1, bottom, jnp.zeros_like(bottom)
+        )
+
+    def chosen(mask):
+        return jnp.where(mask, 1.0, 0.0).astype(jnp.bfloat16)
+
+    def moved(matrix, value):
+        return jnp.dot(matrix, value, preferred_element_type=jnp.float32).astype(jnp.bfloat16)
+
+    few = above.shape[0]
+    pixel = lax.broadcasted_iota(jnp.int32, (tall, few), 0)
+    token = lax.broadcasted_iota(jnp.int32, (tall, few), 1)
+    spread = chosen(token == (pixel // (2 * breadth)) * GRID_W + (pixel % breadth) // 2)
+    frames[2] = moved(spread, above[...].astype(jnp.bfloat16))
+
+    def shifts(size):
+        to = lax.broadcasted_iota(jnp.int32, (size, size), 0)
+        origin = lax.broadcasted_iota(jnp.int32, (size, size), 1)
+        column = to % breadth
+        return (
+            chosen((origin == to - 1) & (column > 0)),
+            chosen((origin == to + 1) & (column < breadth - 1)),
+        )
+
+    left, right = shifts(tall)
+    for t in range(3):
+        wide[t, :, :channels] = moved(left, frames[t])
+        wide[t, :, channels : 2 * channels] = frames[t]
+        wide[t, :, 2 * channels :] = moved(right, frames[t])
+    extended = count + 2 * breadth
+    first = jnp.zeros((extended, channels), jnp.float32) + bias_time[...]
+    for t in range(3):
+        for dy in range(3):
+            first = first + jnp.dot(
+                wide[t, dy * breadth : dy * breadth + extended, :],
+                w_time[3 * t + dy],
+                preferred_element_type=jnp.float32,
+            )
+    row = tile * (count // breadth) - 1 + lax.broadcasted_iota(
+        jnp.int32, (extended, channels), 0
+    ) // breadth
+    inside = (row >= 0) & (row < tiles * (count // breadth))
+    active = jnp.where(inside, silu(first), 0.0).astype(jnp.bfloat16)
+    left, right = shifts(extended)
+    wide_active[:, :channels] = moved(left, active)
+    wide_active[:, channels : 2 * channels] = active
+    wide_active[:, 2 * channels :] = moved(right, active)
+    total = frames[2, edge : edge + count, :].astype(jnp.float32) + bias_space[...]
+    for dy in range(3):
+        total = total + jnp.dot(
+            wide_active[dy * breadth : dy * breadth + count, :],
+            w_space[dy],
+            preferred_element_type=jnp.float32,
+        )
+    out[...] = total.astype(jnp.bfloat16)
+
+
+def decode(coarse, past, halo, w_time, bias_time, w_space, bias_space, tiles):
+    count, channels = past.shape[1:]
+    breadth = 2 * GRID_W
+    tall = count + 2 * HALO * breadth
+    few = coarse.shape[0] // tiles + 2 * GRID_W
+    return pl.pallas_call(
+        conv_kernel,
+        out_shape=jax.ShapeDtypeStruct((count, channels), jnp.bfloat16),
+        in_specs=[VMEM] * 7,
+        out_specs=VMEM,
+        scratch_shapes=[
+            pltpu.VMEM((few, channels), jnp.float32),
+            pltpu.VMEM((3, tall, channels), jnp.bfloat16),
+            pltpu.VMEM((3, tall, 3 * channels), jnp.bfloat16),
+            pltpu.VMEM((count + 2 * breadth, 3 * channels), jnp.bfloat16),
+        ],
+        compiler_params=pltpu.CompilerParams(vmem_limit_bytes=24 * 2**20),
+        name="decode",
+    )(coarse, past, halo, w_time, bias_time, w_space, bias_space)
+
+
+def dispatch(outgoing, past, w_gate, w_up, w_down, sessions, tiles, cap):
+    slots, (hid, width) = outgoing.shape[0], w_gate.shape
+    hbm = pl.BlockSpec(memory_space=pl.ANY)
     return pl.pallas_call(
         functools.partial(dispatch_kernel, sessions, tiles, cap),
-        out_shape=jax.ShapeDtypeStruct(outgoing.shape, outgoing.dtype),
-        in_specs=[VMEM],
-        out_specs=VMEM,
+        out_shape=(
+            jax.ShapeDtypeStruct(outgoing.shape, outgoing.dtype),
+            jax.ShapeDtypeStruct((2, 2, HALO) + past.shape[2:], past.dtype),
+        ),
+        in_specs=[VMEM, VMEM, hbm, hbm, hbm],
+        out_specs=(VMEM, VMEM),
         scratch_shapes=[
+            pltpu.VMEM(outgoing.shape, outgoing.dtype),
+            pltpu.VMEM((hid, width), jnp.bfloat16),
+            pltpu.VMEM((hid, width), jnp.bfloat16),
+            pltpu.VMEM((hid, width), jnp.bfloat16),
+            pltpu.VMEM((slots, hid), jnp.float32),
+            pltpu.VMEM((slots, hid), jnp.float32),
+            pltpu.VMEM((slots, hid), jnp.bfloat16),
             pltpu.SemaphoreType.DMA,
+            pltpu.SemaphoreType.DMA((3,)),
+            pltpu.SemaphoreType.DMA((2,)),
+            pltpu.SemaphoreType.DMA((2,)),
             pltpu.SemaphoreType.DMA((sessions,)),
             pltpu.SemaphoreType.DMA((sessions,)),
             pltpu.SemaphoreType.DMA((tiles,)),
             pltpu.SemaphoreType.DMA((tiles,)),
         ],
         compiler_params=pltpu.CompilerParams(
-            collective_id=0, has_side_effects=True, vmem_limit_bytes=30 * 2**20
+            collective_id=0, has_side_effects=True, vmem_limit_bytes=50 * 2**20
         ),
         name="dispatch",
-    )(outgoing)
+    )(outgoing, past, w_gate, w_up, w_down)
 
 
 def bring_back(answer, mix_hi, mix_lo, tokens, gain, w_proj, sessions, tiles, cap):
@@ -237,10 +516,20 @@
     count, channels = tokens.shape[0], w_proj.shape[1]
     return pl.pallas_call(
         functools.partial(return_kernel, sessions, tiles, cap),
-        out_shape=jax.ShapeDtypeStruct((count, channels), jnp.bfloat16),
-        in_specs=[VMEM] * 6,
+        out_shape=jax.ShapeDtypeStruct((count, channels), jnp.float32),
+        in_specs=[
+            VMEM,
+            VMEM,
+            VMEM,
+            pl.BlockSpec(memory_space=pl.ANY),
+            VMEM,
+            pl.BlockSpec(memory_space=pl.ANY),
+        ],
         out_specs=VMEM,
         scratch_shapes=[
+            pltpu.VMEM((count, part), jnp.bfloat16),
+            pltpu.VMEM((part, channels), jnp.bfloat16),
+            pltpu.SemaphoreType.DMA((2,)),
             pltpu.VMEM((tiles - 1, slots, part), jnp.bfloat16),
             pltpu.VMEM((slots, part), jnp.bfloat16),
             pltpu.VMEM((slots, part), jnp.bfloat16),
@@ -260,40 +549,6 @@
     )(answer, mix_hi, mix_lo, tokens, gain, w_proj)
 
 
-def extended(cells, axis, dim, width):
-    count = lax.axis_size(axis)
-    ends = count - 1
-    head = lax.slice_in_dim(cells, 0, width, axis=dim)
-    tail = lax.slice_in_dim(cells, cells.shape[dim] - width, cells.shape[dim], axis=dim)
-    return jnp.concatenate(
-        [
-            lax.ppermute(tail, axis, [(i, i + 1) for i in range(ends)]),
-            cells,
-            lax.ppermute(head, axis, [(i + 1, i) for i in range(ends)]),
-        ],
-        axis=dim,
-    )
-
-
-def slot_targets(routes, capacity):
-    flat = routes.reshape(-1)
-    place = jnp.arange(flat.shape[0], dtype=jnp.int32)
-    earlier = (flat[:, None] == flat[None, :]) & (place[None, :] < place[:, None])
-    return flat * capacity + jnp.sum(earlier.astype(jnp.int32), axis=1)
-
-
-def patches(frames, height):
-    breadth = frames.shape[2]
-    padded = jnp.pad(frames, ((0, 0), (0, 0), (1, 1), (0, 0)))
-    pieces = [
-        padded[t, dy : dy + height, dx : dx + breadth, :]
-        for t in range(frames.shape[0])
-        for dy in range(3)
-        for dx in range(3)
-    ]
-    return jnp.concatenate(pieces, axis=-1).reshape(height * breadth, -1)
-
-
 def body(
     tokens,
     routes,
@@ -311,68 +566,31 @@
     cache_head,
 ):
     sessions, tiles = lax.axis_size("sess"), lax.axis_size("exp")
-    tile = lax.axis_index("exp")
     channels = w_proj.shape[-1]
     local = tokens[0]
     tok_count = local.shape[0]
     cap = 2 * tok_count * TOPK // sessions
     height, breadth = frame_cache.shape[2:4]
-    rows_own = tok_count // tiles
-
-    head = cache_head[0]
-    cache = frame_cache[:, 0]
-    past = jnp.stack(
-        [
-            lax.dynamic_index_in_dim(cache, (head + 2) % 3, 0, keepdims=False),
-            lax.dynamic_index_in_dim(cache, head, 0, keepdims=False),
-        ]
-    )
-    past = extended(past, "exp", 1, HALO)
-
-    dest = slot_targets(routes[0], cap).reshape(tok_count, TOPK)
-    slots = jnp.arange(sessions * cap, dtype=jnp.int32)
-    hit = dest[:, :, None] == slots[None, None, :]
-    onehot = jnp.any(hit, axis=1).astype(jnp.bfloat16)
-    weight = jnp.sum(jnp.where(hit, gates[0][:, :, None], 0.0), axis=1)
-    mix_hi = lax.reduce_precision(weight, 8, 7)
-    mix_lo = (weight - mix_hi).astype(jnp.bfloat16)
-    mix_hi = mix_hi.astype(jnp.bfloat16)
-    outgoing = lax.dot_general(
-        onehot, local, (((0,), (0,)), ((), ())), preferred_element_type=jnp.float32
-    ).astype(jnp.bfloat16)
-
-    rows = dispatch(outgoing, sessions, tiles, cap)
-    gate = jnp.dot(rows, w_gate[0], preferred_element_type=jnp.float32)
-    upward = jnp.dot(rows, w_up[0], preferred_element_type=jnp.float32)
-    hidden = (jax.nn.silu(gate) * upward).astype(jnp.bfloat16)
-    answer = jnp.dot(hidden, w_down[0], preferred_element_type=jnp.float32).astype(jnp.bfloat16)
+    outgoing, mix_hi, mix_lo, past = route(
+        routes[0].T, gates[0].T, local, cache_head, frame_cache[:, 0], sessions, cap
+    )
+    answer, halo = dispatch(
+        outgoing, past, w_gate[0].T, w_up[0].T, w_down[0], sessions, tiles, cap
+    )
     coarse = bring_back(
         answer, mix_hi, mix_lo, local, feat_gain[None, :], w_proj, sessions, tiles, cap
     )
-
-    coarse = jnp.pad(coarse, ((GRID_W, GRID_W), (0, 0)))
-    coarse = lax.dynamic_slice_in_dim(coarse, tile * rows_own, rows_own + 2 * GRID_W, 0)
-    coarse = coarse.reshape(-1, GRID_W, channels)
-    fine = jnp.repeat(jnp.repeat(coarse, 2, axis=0), 2, axis=1)
-    stack = jnp.concatenate([past, fine[None]], axis=0)
-    first = jnp.dot(
-        patches(stack, height + 2),
-        conv_time.reshape(-1, channels),
-        preferred_element_type=jnp.float32,
-    )
-    active = jax.nn.silu(first + bias_time).astype(jnp.bfloat16)
-    active = active.reshape(height + 2, breadth, channels)
-    row = tile * height - 1 + jnp.arange(height + 2, dtype=jnp.int32)
-    inside = (row >= 0) & (row < height * tiles)
-    active = jnp.where(inside[:, None, None], active, jnp.zeros_like(active))
-    second = jnp.dot(
-        patches(active[None], height),
-        conv_space.reshape(-1, channels),
-        preferred_element_type=jnp.float32,
-    )
-    own = fine[HALO : HALO + height].reshape(-1, channels)
-    result = own.astype(jnp.float32) + second + bias_space
-    return result.astype(jnp.bfloat16).reshape(1, height, breadth, channels)
+    result = decode(
+        coarse,
+        past.reshape(2, height * breadth, channels),
+        halo.reshape(2, 2, HALO * breadth, channels),
+        conv_time.reshape(9, 3 * channels, channels),
+        bias_time[None, :],
+        conv_space.reshape(3, 3 * channels, channels),
+        bias_space[None, :],
+        tiles,
+    )
+    return result.reshape(1, height, breadth, channels)
 
 
 def solution(mesh):

time: 134 us -> 92.6 us (0.69)
  matrix products: 22.2 us -> 0 us
  local copies, waits for them, and re-layouts: 21.8 us -> 4.68 us
  Pallas kernels: 74.3 us -> 86.9 us
  starting transfers between devices: 6.77 us -> 0 us
  other arithmetic: 6.55 us -> 0 us
    dot_general x5 -> x0, matrix products: 22.2 us -> none  [the longest x1 12.8 us: body(): jnp.dot(hidden, w_down[0], preferred_element_type=jnp.float32)]
    pallas_call x1, Pallas kernels: 38.8 us -> 47.7 us  [dispatch(): pl.pallas_call(functools.partial(dispatch_kernel, sessions, tiles, cap),...]
    ppermute x2 -> x0, starting transfers between devices: 6.77 us -> none  [the longest x1 5.49 us: extended(): lax.ppermute(tail, axis, [(i, i + 1) for i in range(ends)])]
    unnamed x77 -> x24, local copies, waits for them, and re-layouts: 10.9 us -> 4.68 us
    pallas_call x0 -> x2, Pallas kernels: none -> 3.33 us  [the longest x1 2.49 us: decode(): pl.pallas_call(conv_kernel, out_shape=jax.ShapeDtypeStruct((count, channe...]
    concatenate x3 -> x0, other arithmetic: 2.83 us -> none  [the longest x2 1.62 us: extended(): jnp.concatenate([lax.ppermute(tail, axis, [(i, i + 1) for i in range(ends...]
    broadcast_in_dim x4 -> x0, local copies, waits for them, and re-layouts: 2.15 us -> none  [body(): fine = jnp.repeat(jnp.repeat(coarse, 2, axis=0), 2, axis=1)]
    slice x4 -> x0, local copies, waits for them, and re-layouts: 1.96 us -> none  [patches(): padded[t, dy:dy + height, dx:dx + breadth, :]]
  transfers between devices with their start and end apart: 2 -> 0, of which waited for: 0 -> 0; matrix products, arithmetic and copies ran while one was open for 26% -> 0% of each run, Pallas kernels for 56% -> 0%
where the time goes in v2:
time: 92.6 us; the launch traced here: 92.4 us
  Pallas kernels  86.9 us (94%)
  local copies, waits for them, and re-layouts  4.68 us (5%)
    pallas_call x1, Pallas kernels, dispatch(): pl.pallas_call(functools.partial(dispatch_kernel, sessions, tiles, cap),...  47.7 us
    pallas_call x1, Pallas kernels, bring_back(): pl.pallas_call(functools.partial(return_kernel, sessions, tiles, cap), ou...  35.9 us
    unnamed x24, local copies, waits for them, and re-layouts  4.68 us
    pallas_call x1, Pallas kernels, decode(): pl.pallas_call(conv_kernel, out_shape=jax.ShapeDtypeStruct((count, channe...  2.49 us

profile of v2, /device:TPU:0, one launch (start us, length us, event | category | flops | bytes accessed | tf_op | source)
XLA Modules:
  0.0 92.4 jit_solution(16556620841487417727)
XLA Ops:
  0.7 0.0 copy-start.3
  0.7 1.0 %copy-done.3 = bf16[1,64,4096]{2,1,0:T(8,128)(2,1)S(1)} copy-done((bf16[1,64,4096]{2,1,0:T(8,128)(2,1)S(1)}, bf16[1,64,4096]{2,1,0:T(8,128)(2,1)}, u32[]{:S(2)}) %copy-start.3) | copy-done | bytes 524312
  1.7 0.0 copy-start.6
  1.7 0.9 %copy-done.6 = bf16[3,1,8,16,256]{4,3,2,1,0:T(8,128)(2,1)S(1)} copy-done((bf16[3,1,8,16,256]{4,3,2,1,0:T(8,128)(2,1)S(1)}, bf16[3,1,8,16,256]{4,3,2,1,0:T(8,128)(2,1)}, u32[]{:S(2)}) %copy-start.6) | copy-done | bytes 196632
  2.6 0.0 copy-start.8
  2.6 0.7 copy-done.8
  3.3 0.0 copy-start.9
  3.3 0.7 copy-done.9
  4.0 0.8 route.1
  4.8 0.0 copy-start.1
  4.8 1.3 %copy-done.1 = bf16[256,4096]{1,0:T(8,128)(2,1)} copy-done((bf16[256,4096]{1,0:T(8,128)(2,1)}, bf16[256,4096]{1,0:T(8,128)(2,1)S(1)}, u32[]{:S(2)}) %copy-start.1) | copy-done | bytes 2097176
  6.2 0.0 copy-start.2
  6.2 0.0 copy-start.4
  6.2 0.0 copy-start.7
  6.2 47.7 %dispatch.1 = (bf16[256,4096]{1,0:T(8,128)(2,1)S(1)}, bf16[2,2,2,16,256]{4,3,2,1,0:T(8,128)(2,1)S(1)}) custom-call(bf16[256,4096]{1,0:T(8,128)(2,1)} %copy-done.1, bf16[2,8,16,256]{3,2,1,0:T(8,128)(2,1)S(1)} %get-tuple-element.12.past, bf16[704,4096]{1,0:T(8,128)(2,1)} %bitcast.35, bf16[704,4096]{1,0:T(8,128)(2,1)} %bitcast.36, bf16[704,4096]{1,0:T(8,128)(2,1)} %bitcast.37), custom_call_target="tpu_custom_call" | custom-call | tf_op jit(solution)/shard_map/dispatch/pallas_call | solution.py:481
  53.9 0.0 copy-start
  53.9 0.0 copy-start.5
  53.9 0.0 copy-start.10
  53.9 0.0 copy-start.11
  53.9 0.0 copy-done.2
  53.9 0.0 copy-done.4
  53.9 0.0 copy-done.7
  54.0 35.9 %bring_back.1.coarse = f32[64,256]{1,0:T(8,128)S(1)} custom-call(bf16[256,4096]{1,0:T(8,128)(2,1)S(1)} %get-tuple-element.13.answer, bf16[64,256]{1,0:T(8,128)(2,1)S(1)} %get-tuple-element.14.mix_hi, bf16[64,256]{1,0:T(8,128)(2,1)S(1)} %get-tuple-element.15.mix_lo, bf16[64,4096]{1,0:T(8,128)(2,1)S(1)} %bitcast.25, f32[1,4096]{1,0:T(1,128)S(1)} %bitcast.30, ...), custom_call_target="tpu_custom_call" | custom-call | tf_op jit(solution)/shard_map/bring_back/pallas_call | solution.py:517
  89.9 0.0 copy-done
  89.9 0.0 copy-done.5
  89.9 0.0 copy-done.10
  89.9 0.0 copy-done.11
  89.9 2.5 %decode.1 = bf16[128,256]{1,0:T(8,128)(2,1)} custom-call(f32[64,256]{1,0:T(8,128)S(1)} %bring_back.1.coarse, bf16[2,128,256]{2,1,0:T(8,128)(2,1)S(1)} %bitcast.27, bf16[2,2,32,256]{3,2,1,0:T(8,128)(2,1)S(1)} %bitcast.29, bf16[9,768,256]{2,1,0:T(8,128)(2,1)S(1)} %bitcast.23, f32[1,256]{1,0:T(1,128)S(1)} %bitcast.33, bf16[3,768,256]{2,1,0:T(8,128)(2,1)S(1)} %bitcast.26, ...), custom_call_target="tpu_custom_call" | custom-call | tf_op jit(solution)/shard_map/decode/pallas_call | solution.py:462
Async XLA Ops:
  0.7 1.0 %copy-start.3 = (bf16[1,64,4096]{2,1,0:T(8,128)(2,1)S(1)}, bf16[1,64,4096]{2,1,0:T(8,128)(2,1)}, u32[]{:S(2)}) copy-start(bf16[1,64,4096]{2,1,0:T(8,128)(2,1)} %param.14) | copy-start | bytes 1572868
  1.7 0.9 %copy-start.6 = (bf16[3,1,8,16,256]{4,3,2,1,0:T(8,128)(2,1)S(1)}, bf16[3,1,8,16,256]{4,3,2,1,0:T(8,128)(2,1)}, u32[]{:S(2)}) copy-start(bf16[3,1,8,16,256]{4,3,2,1,0:T(8,128)(2,1)} %param.26) | copy-start | bytes 589828
  2.6 0.7 copy-start.8
  3.3 0.7 copy-start.9
  4.8 1.3 %copy-start.1 = (bf16[256,4096]{1,0:T(8,128)(2,1)}, bf16[256,4096]{1,0:T(8,128)(2,1)S(1)}, u32[]{:S(2)}) copy-start(bf16[256,4096]{1,0:T(8,128)(2,1)S(1)} %get-tuple-element.11.src) | copy-start | bytes 6291460
  6.2 47.8 %copy-start.2 = (bf16[4096,256]{1,0:T(8,128)(2,1)S(1)}, bf16[4096,256]{1,0:T(8,128)(2,1)}, u32[]{:S(2)}) copy-start(bf16[4096,256]{1,0:T(8,128)(2,1)} %all_proj.1) | copy-start | bytes 6291460
  6.2 47.8 %copy-start.4 = (bf16[1,64,4096]{2,1,0:T(8,128)(2,1)S(1)}, bf16[1,64,4096]{2,1,0:T(8,128)(2,1)}, u32[]{:S(2)}) copy-start(bf16[1,64,4096]{2,1,0:T(8,128)(2,1)} %param.14) | copy-start | bytes 1572868
  6.2 47.8 %copy-start.7 = (f32[4096]{0:T(1024)S(1)}, f32[4096]{0:T(1024)}, u32[]{:S(2)}) copy-start(f32[4096]{0:T(1024)} %param.20) | copy-start | bytes 49156
  53.9 36.0 %copy-start = (bf16[3,3,3,256,256]{4,3,2,1,0:T(8,128)(2,1)S(1)}, bf16[3,3,3,256,256]{4,3,2,1,0:T(8,128)(2,1)}, u32[]{:S(2)}) copy-start(bf16[3,3,3,256,256]{4,3,2,1,0:T(8,128)(2,1)} %param.22) | copy-start | bytes 10616836
  53.9 36.0 %copy-start.5 = (bf16[3,3,256,256]{3,2,1,0:T(8,128)(2,1)S(1)}, bf16[3,3,256,256]{3,2,1,0:T(8,128)(2,1)}, u32[]{:S(2)}) copy-start(bf16[3,3,256,256]{3,2,1,0:T(8,128)(2,1)} %param.24) | copy-start | bytes 3538948
  53.9 36.0 %copy-start.10 = (f32[256]{0:T(256)S(1)}, f32[256]{0:T(256)}, u32[]{:S(2)}) copy-start(f32[256]{0:T(256)} %param.23) | copy-start | bytes 3076
  53.9 36.0 %copy-start.11 = (f32[256]{0:T(256)S(1)}, f32[256]{0:T(256)}, u32[]{:S(2)}) copy-start(f32[256]{0:T(256)} %param.25) | copy-start | bytes 3076

commit v3 on v2

--- a/solution.py
+++ b/solution.py
@@ -10,6 +10,7 @@
 TOPK = 2
 GRID_W = 8
 HALO = 2
+DIRECT = 4
 MESH = pl.DeviceIdType.MESH
 VMEM = pl.BlockSpec(memory_space=pltpu.VMEM)
 
@@ -106,7 +107,7 @@
     copies = {}
     for k in order:
         other = partner(me, k)
-        span = slice(None) if k == 1 else columns
+        span = slice(None) if k < DIRECT else columns
         copies[k] = pltpu.make_async_remote_copy(
             src_ref=src.at[rows(other), span],
             dst_ref=out.at[rows(me), span],
@@ -132,7 +133,7 @@
         borders[-1].start()
     for k in order:
         copies[k].wait_recv()
-        if k == 1:
+        if k < DIRECT:
             continue
         block = out.at[rows(partner(me, k)), columns]
         for m in range(1, tiles):
@@ -147,7 +148,7 @@
     for k in order:
         copies[k].wait_send()
     own.wait()
-    passed = out.at[pl.ds(0, (len(order) - 1) * cap), columns]
+    passed = out.at[pl.ds(0, (sessions - DIRECT) * cap), columns]
     for m in range(1, tiles):
         pltpu.make_async_copy(passed, passed, send2.at[m]).wait()
         pltpu.make_async_copy(passed, passed, recv2.at[m]).wait()
@@ -308,12 +309,40 @@
 
 
 def route_kernel(
-    sessions, cap, routes, gates, tokens, head, cache, outgoing, mix_hi, mix_lo, past
+    sessions,
+    cap,
+    all_routes,
+    all_gates,
+    all_tokens,
+    head,
+    cache,
+    outgoing,
+    mix_hi,
+    mix_lo,
+    past,
+    routes,
+    gates,
+    tokens,
+    sems,
 ):
     count = tokens.shape[0]
     slots = sessions * cap
-    past[1] = cache[head[0]]
-    past[0] = cache[lax.rem(head[0] + 2, 3)]
+    loads = [
+        pltpu.make_async_copy(source, held, sems.at[i])
+        for i, (source, held) in enumerate(
+            (
+                (all_routes, routes),
+                (all_gates, gates),
+                (all_tokens, tokens),
+                (cache.at[head[0]], past.at[1]),
+                (cache.at[lax.rem(head[0] + 2, 3)], past.at[0]),
+            )
+        )
+    ]
+    for load in loads:
+        load.start()
+    for load in loads:
+        load.wait()
     expert = lax.broadcasted_iota(jnp.int32, (sessions, count), 0)
     named = [(routes[k : k + 1, :] == expert).astype(jnp.float32) for k in range(TOPK)]
     earlier = lax.broadcasted_iota(jnp.int32, (count, count), 0) < lax.broadcasted_iota(
@@ -348,6 +377,7 @@
 def route(routes, gates, tokens, head, cache, sessions, cap):
     slots, count = sessions * cap, tokens.shape[0]
     mix = jax.ShapeDtypeStruct((count, slots), jnp.bfloat16)
+    hbm = pl.BlockSpec(memory_space=pltpu.HBM)
     return pl.pallas_call(
         functools.partial(route_kernel, sessions, cap),
         out_shape=(
@@ -356,9 +386,15 @@
             mix,
             jax.ShapeDtypeStruct((2,) + cache.shape[1:], cache.dtype),
         ),
-        in_specs=[VMEM, VMEM, VMEM, pl.BlockSpec(memory_space=pltpu.SMEM), VMEM],
+        in_specs=[hbm, hbm, hbm, pl.BlockSpec(memory_space=pltpu.SMEM), hbm],
         out_specs=(VMEM,) * 4,
-        compiler_params=pltpu.CompilerParams(vmem_limit_bytes=30 * 2**20),
+        scratch_shapes=[
+            pltpu.VMEM(routes.shape, routes.dtype),
+            pltpu.VMEM(gates.shape, gates.dtype),
+            pltpu.VMEM(tokens.shape, tokens.dtype),
+            pltpu.SemaphoreType.DMA((5,)),
+        ],
+        compiler_params=pltpu.CompilerParams(vmem_limit_bytes=56 * 2**20),
         name="route",
     )(routes, gates, tokens, head, cache)
 

time: 92.6 us -> 91.3 us (0.986)
  local copies, waits for them, and re-layouts: 4.68 us -> 0.95 us
  Pallas kernels: 86.9 us -> 89.4 us
    unnamed x24 -> x22, local copies, waits for them, and re-layouts: 4.68 us -> 0.95 us
    pallas_call x1, Pallas kernels: 0.83 us -> 3.28 us  [route(): pl.pallas_call(functools.partial(route_kernel, sessions, cap), out_shape=...]
where the time goes in v3:
time: 91.3 us; the launch traced here: 91.2 us
  Pallas kernels  89.4 us (98%)
  local copies, waits for them, and re-layouts  0.95 us (1%)
    pallas_call x1, Pallas kernels, dispatch(): pl.pallas_call(functools.partial(dispatch_kernel, sessions, tiles, cap),...  47.7 us
    pallas_call x1, Pallas kernels, bring_back(): pl.pallas_call(functools.partial(return_kernel, sessions, tiles, cap), ou...  35.9 us
    pallas_call x1, Pallas kernels, route(): pl.pallas_call(functools.partial(route_kernel, sessions, cap), out_shape=...  3.28 us
    pallas_call x1, Pallas kernels, decode(): pl.pallas_call(conv_kernel, out_shape=jax.ShapeDtypeStruct((count, channe...  2.49 us

profile of v3, /device:TPU:0, one launch (start us, length us, event | category | flops | bytes accessed | tf_op | source)
XLA Modules:
  0.0 91.2 jit_solution(17459193407938283942)
XLA Ops:
  0.7 3.3 %route.1 = (bf16[256,4096]{1,0:T(8,128)(2,1)}, bf16[64,256]{1,0:T(8,128)(2,1)}, bf16[64,256]{1,0:T(8,128)(2,1)}, bf16[2,8,16,256]{3,2,1,0:T(8,128)(2,1)}) custom-call(s32[2,64]{1,0:T(2,128)} %bitcast.36, f32[2,64]{1,0:T(2,128)} %bitcast.37, bf16[64,4096]{1,0:T(8,128)(2,1)} %bitcast.24, s32[1]{0:T(128)S(6)} %copy.15.head, bf16[3,8,16,256]{3,2,1,0:T(8,128)(2,1)} %bitcast.35), custom_call_target="tpu_custom_call" | custom-call | tf_op jit(solution)/shard_map/route/pallas_call | solution.py:381
  3.9 0.0 copy-start.4
  4.0 0.9 copy-done.4
  4.8 0.0 copy-start.1
  4.9 0.0 copy-start.2
  4.9 0.0 copy-start.6
  4.9 0.0 copy-start.7
  4.9 0.0 copy-start.8
  4.9 47.7 %dispatch.1 = (bf16[256,4096]{1,0:T(8,128)(2,1)S(1)}, bf16[2,2,2,16,256]{4,3,2,1,0:T(8,128)(2,1)S(1)}) custom-call(bf16[256,4096]{1,0:T(8,128)(2,1)} %get-tuple-element.11.src, bf16[2,8,16,256]{3,2,1,0:T(8,128)(2,1)S(1)} %copy-done.4, bf16[704,4096]{1,0:T(8,128)(2,1)} %bitcast.32, bf16[704,4096]{1,0:T(8,128)(2,1)} %bitcast.33, bf16[704,4096]{1,0:T(8,128)(2,1)} %bitcast.34), custom_call_target="tpu_custom_call" | custom-call | tf_op jit(solution)/shard_map/dispatch/pallas_call | solution.py:517
  52.6 0.0 copy-start
  52.6 0.0 copy-start.3
  52.6 0.0 copy-start.5
  52.6 0.0 copy-start.9
  52.7 0.0 copy-start.10
  52.7 0.0 copy-done.1
  52.7 0.0 copy-done.2
  52.7 0.0 copy-done.6
  52.7 0.0 copy-done.7
  52.7 0.0 copy-done.8
  52.7 35.9 %bring_back.1.coarse = f32[64,256]{1,0:T(8,128)S(1)} custom-call(bf16[256,4096]{1,0:T(8,128)(2,1)S(1)} %get-tuple-element.13.answer, bf16[64,256]{1,0:T(8,128)(2,1)S(1)} %copy-done.6, bf16[64,256]{1,0:T(8,128)(2,1)S(1)} %copy-done.7, bf16[64,4096]{1,0:T(8,128)(2,1)S(1)} %bitcast.25, f32[1,4096]{1,0:T(1,128)S(1)} %bitcast.29, bf16[4096,256]{1,0:T(8,128)(2,1)S(1)} %copy-done.1), custom_call_target="tpu_custom_call" | custom-call | tf_op jit(solution)/shard_map/bring_back/pallas_call | solution.py:553
  88.6 0.0 copy-done
  88.6 0.0 copy-done.3
  88.6 0.0 copy-done.5
  88.6 0.0 copy-done.9
  88.6 0.0 copy-done.10
  88.7 2.5 %decode.1 = bf16[128,256]{1,0:T(8,128)(2,1)} custom-call(f32[64,256]{1,0:T(8,128)S(1)} %bring_back.1.coarse, bf16[2,128,256]{2,1,0:T(8,128)(2,1)S(1)} %bitcast.27, bf16[2,2,32,256]{3,2,1,0:T(8,128)(2,1)S(1)} %bitcast.28, bf16[9,768,256]{2,1,0:T(8,128)(2,1)S(1)} %bitcast.23, f32[1,256]{1,0:T(1,128)S(1)} %bitcast.30, bf16[3,768,256]{2,1,0:T(8,128)(2,1)S(1)} %bitcast.26, ...), custom_call_target="tpu_custom_call" | custom-call | tf_op jit(solution)/shard_map/decode/pallas_call | solution.py:498
Async XLA Ops:
  3.9 0.9 copy-start.4
  4.8 47.8 %copy-start.1 = (bf16[4096,256]{1,0:T(8,128)(2,1)S(1)}, bf16[4096,256]{1,0:T(8,128)(2,1)}, u32[]{:S(2)}) copy-start(bf16[4096,256]{1,0:T(8,128)(2,1)} %all_proj.1) | copy-start | bytes 6291460
  4.9 47.8 %copy-start.2 = (bf16[1,64,4096]{2,1,0:T(8,128)(2,1)S(1)}, bf16[1,64,4096]{2,1,0:T(8,128)(2,1)}, u32[]{:S(2)}) copy-start(bf16[1,64,4096]{2,1,0:T(8,128)(2,1)} %param.14) | copy-start | bytes 1572868
  4.9 47.8 %copy-start.6 = (bf16[64,256]{1,0:T(8,128)(2,1)S(1)}, bf16[64,256]{1,0:T(8,128)(2,1)}, u32[]{:S(2)}) copy-start(bf16[64,256]{1,0:T(8,128)(2,1)} %get-tuple-element.14.mix_hi) | copy-start | bytes 98308
  4.9 47.8 %copy-start.7 = (bf16[64,256]{1,0:T(8,128)(2,1)S(1)}, bf16[64,256]{1,0:T(8,128)(2,1)}, u32[]{:S(2)}) copy-start(bf16[64,256]{1,0:T(8,128)(2,1)} %get-tuple-element.15.mix_lo) | copy-start | bytes 98308
  4.9 47.8 %copy-start.8 = (f32[4096]{0:T(1024)S(1)}, f32[4096]{0:T(1024)}, u32[]{:S(2)}) copy-start(f32[4096]{0:T(1024)} %param.20) | copy-start | bytes 49156
  52.6 36.0 %copy-start = (bf16[3,3,3,256,256]{4,3,2,1,0:T(8,128)(2,1)S(1)}, bf16[3,3,3,256,256]{4,3,2,1,0:T(8,128)(2,1)}, u32[]{:S(2)}) copy-start(bf16[3,3,3,256,256]{4,3,2,1,0:T(8,128)(2,1)} %param.22) | copy-start | bytes 10616836
  52.6 36.0 %copy-start.3 = (bf16[3,3,256,256]{3,2,1,0:T(8,128)(2,1)S(1)}, bf16[3,3,256,256]{3,2,1,0:T(8,128)(2,1)}, u32[]{:S(2)}) copy-start(bf16[3,3,256,256]{3,2,1,0:T(8,128)(2,1)} %param.24) | copy-start | bytes 3538948
  52.6 36.0 %copy-start.5 = (bf16[2,8,16,256]{3,2,1,0:T(8,128)(2,1)S(1)}, bf16[2,8,16,256]{3,2,1,0:T(8,128)(2,1)}, u32[]{:S(2)}) copy-start(bf16[2,8,16,256]{3,2,1,0:T(8,128)(2,1)} %get-tuple-element.12.past) | copy-start | bytes 393220
  52.6 36.0 %copy-start.9 = (f32[256]{0:T(256)S(1)}, f32[256]{0:T(256)}, u32[]{:S(2)}) copy-start(f32[256]{0:T(256)} %param.23) | copy-start | bytes 3076
  52.7 36.0 %copy-start.10 = (f32[256]{0:T(256)S(1)}, f32[256]{0:T(256)}, u32[]{:S(2)}) copy-start(f32[256]{0:T(256)} %param.25) | copy-start | bytes 3076
